TPU v7x, 64 devices: a 2x2x8 block of a 4x4x8 slice. The times are simulated.
64 devices in a mesh: dp: 4 (over x, y), tp: 16 (over z, core).
Axes of the slice: x: 2, y: 2, z: 8, core: 2. Of those that a mesh axis runs over, the one named last changes fastest.
The devices are a block of a 4x4x8 slice.
Arguments:
- layer_in: bfloat16 [16384, 1024], P(('dp', 'tp')), parts along dimension 0
- resid_mid: bfloat16 [16384, 1024], P(('dp', 'tp')), parts along dimension 0
- grad_out: bfloat16 [16384, 1024], P(('dp', 'tp')), parts along dimension 0
- ln1_gain: float32 [1024], replicated
- ln2_gain: float32 [1024], replicated
- w_qkv: bfloat16 [1024, 3072], P(None, 'tp')
- w_out: bfloat16 [16, 64, 1024], P('tp')
- w_fc1: bfloat16 [1024, 4096], P(None, 'tp')
- w_fc2: bfloat16 [4096, 1024], P('tp')
Outputs:
- output 1: bfloat16 [16384, 1024], P(('dp', 'tp')), parts along dimension 0
- output 2: bfloat16 [4096, 3072], P('dp', 'tp'), parts along dimension 0
- output 3: bfloat16 [64, 64, 1024], P(('dp', 'tp')), parts along dimension 0
- output 4: bfloat16 [4096, 4096], P('dp', 'tp'), parts along dimension 0
- output 5: bfloat16 [16384, 1024], P(('dp', 'tp')), parts along dimension 0
There are 4 independent parts. A program takes and returns all parts, laid end to end along the dimension named above; an argument that names none is the same for every part.
All inputs are finite; a program needn't handle non-finite values.
Results may differ from a plain program's by a relative error of at most 0.0175564.
Values are sent between devices in bfloat16 or wider.
A program may use at most 768 MiB of HBM per device.

v0:
```python
import jax
import jax.numpy as jnp
from jax import lax
from jax.sharding import PartitionSpec as P, NamedSharding

LN_EPS = 1e-5
GELU_COEF = 0.044715
GELU_SCALE = 0.7978845608028654


def ln_forward(rows):
    row_mean = jnp.mean(rows, axis=-1, keepdims=True)
    centered = rows - row_mean
    row_rstd = lax.rsqrt(jnp.mean(centered * centered, axis=-1, keepdims=True) + LN_EPS)
    return centered * row_rstd, row_rstd


def ln_backward(x_hat, row_rstd, ln_gain, grad_norm):
    grad_hat = grad_norm * ln_gain
    proj_one = jnp.mean(grad_hat, axis=-1, keepdims=True)
    proj_two = jnp.mean(grad_hat * x_hat, axis=-1, keepdims=True)
    return row_rstd * (grad_hat - proj_one - x_hat * proj_two)


def gelu_pair(pre_act):
    tanh_val = jnp.tanh(GELU_SCALE * (pre_act + GELU_COEF * pre_act * pre_act * pre_act))
    gelu_val = 0.5 * pre_act * (1.0 + tanh_val)
    gelu_der = 0.5 * (1.0 + tanh_val) + 0.5 * pre_act * (1.0 - tanh_val * tanh_val) * GELU_SCALE * (1.0 + 3.0 * GELU_COEF * pre_act * pre_act)
    return gelu_val, gelu_der


def attention_grads(norm_rows, grad_mid_rows, wqkv_part, wout_part):
    tokens = norm_rows.shape[0]
    heads_loc = wout_part.shape[0]
    head_dim = wout_part.shape[1]
    score_scale = head_dim ** -0.5
    qkv_rows = jnp.dot(norm_rows, wqkv_part, preferred_element_type=jnp.float32).astype(jnp.bfloat16)
    qkv_rows = qkv_rows.reshape(tokens, heads_loc, 3, head_dim)
    q_rows = qkv_rows[:, :, 0]
    k_rows = qkv_rows[:, :, 1]
    v_rows = qkv_rows[:, :, 2]
    scores = jnp.einsum('qnd,knd->nqk', q_rows, k_rows, preferred_element_type=jnp.float32) * score_scale
    causal = jnp.arange(tokens)[:, None] >= jnp.arange(tokens)[None, :]
    attn_prob = jax.nn.softmax(jnp.where(causal, scores, -1e30), axis=-1)
    prob_low = attn_prob.astype(jnp.bfloat16)
    attn_out = jnp.einsum('nqk,knd->qnd', prob_low, v_rows, preferred_element_type=jnp.float32).astype(jnp.bfloat16)
    grad_attn = jnp.einsum('tm,ndm->tnd', grad_mid_rows, wout_part, preferred_element_type=jnp.float32).astype(jnp.bfloat16)
    grad_v = jnp.einsum('nqk,qnd->knd', prob_low, grad_attn, preferred_element_type=jnp.float32).astype(jnp.bfloat16)
    grad_prob = jnp.einsum('qnd,knd->nqk', grad_attn, v_rows, preferred_element_type=jnp.float32)
    row_dot = jnp.sum(attn_prob * grad_prob, axis=-1, keepdims=True)
    grad_score = (attn_prob * (grad_prob - row_dot) * score_scale).astype(jnp.bfloat16)
    grad_q = jnp.einsum('nqk,knd->qnd', grad_score, k_rows, preferred_element_type=jnp.float32).astype(jnp.bfloat16)
    grad_k = jnp.einsum('nqk,qnd->knd', grad_score, q_rows, preferred_element_type=jnp.float32).astype(jnp.bfloat16)
    grad_qkv = jnp.stack([grad_q, grad_k, grad_v], axis=2).reshape(tokens, 3 * heads_loc * head_dim)
    return attn_out, grad_qkv


def solution(mesh):
    row_spec = P(('dp', 'tp'), None)
    in_specs = (row_spec, row_spec, row_spec, P(None), P(None), P(None, 'tp'), P('tp', None, None), P(None, 'tp'), P('tp', None))
    out_specs = (row_spec, P('dp', 'tp'), P(('dp', 'tp'), None, None), P('dp', 'tp'), P(('dp', 'tp'), None))

    def device_step(in_rows, mid_rows, gout_rows, ln1_gain, ln2_gain, wqkv_loc, wout_loc, wfc1_loc, wfc2_loc):
        mid_hat, mid_rstd = ln_forward(mid_rows.astype(jnp.float32))
        ln2_loc = (mid_hat * ln2_gain).astype(jnp.bfloat16)
        ln2_all = lax.all_gather(ln2_loc, 'tp', axis=0, tiled=True)
        gout_all = lax.all_gather(gout_rows, 'tp', axis=0, tiled=True)
        pre_act = jnp.dot(ln2_all, wfc1_loc, preferred_element_type=jnp.float32)
        gelu_val, gelu_der = gelu_pair(pre_act)
        act_low = gelu_val.astype(jnp.bfloat16)
        grad_wfc2 = jnp.einsum('tf,tm->fm', act_low, gout_all, preferred_element_type=jnp.float32).astype(jnp.bfloat16)
        grad_act = jnp.einsum('tm,fm->tf', gout_all, wfc2_loc, preferred_element_type=jnp.float32)
        grad_pre = (grad_act * gelu_der).astype(jnp.bfloat16)
        grad_wfc1 = jnp.einsum('tm,tf->mf', ln2_all, grad_pre, preferred_element_type=jnp.float32).astype(jnp.bfloat16)
        norm2_part = jnp.einsum('tf,mf->tm', grad_pre, wfc1_loc, preferred_element_type=jnp.float32).astype(jnp.bfloat16)
        grad_norm2 = lax.psum_scatter(norm2_part, 'tp', scatter_dimension=0, tiled=True)
        grad_mid = gout_rows.astype(jnp.float32) + ln_backward(mid_hat, mid_rstd, ln2_gain, grad_norm2.astype(jnp.float32))
        in_hat, in_rstd = ln_forward(in_rows.astype(jnp.float32))
        ln1_loc = (in_hat * ln1_gain).astype(jnp.bfloat16)
        ln1_all = lax.all_gather(ln1_loc, 'tp', axis=0, tiled=True)
        grad_mid_all = lax.all_gather(grad_mid.astype(jnp.bfloat16), 'tp', axis=0, tiled=True)
        attn_out, grad_qkv = attention_grads(ln1_all, grad_mid_all, wqkv_loc, wout_loc)
        grad_wout = jnp.einsum('tnd,tm->ndm', attn_out, grad_mid_all, preferred_element_type=jnp.float32).astype(jnp.bfloat16)
        grad_wqkv = jnp.einsum('tm,tc->mc', ln1_all, grad_qkv, preferred_element_type=jnp.float32).astype(jnp.bfloat16)
        norm1_part = jnp.einsum('tc,mc->tm', grad_qkv, wqkv_loc, preferred_element_type=jnp.float32).astype(jnp.bfloat16)
        grad_norm1 = lax.psum_scatter(norm1_part, 'tp', scatter_dimension=0, tiled=True)
        grad_in = (grad_mid + ln_backward(in_hat, in_rstd, ln1_gain, grad_norm1.astype(jnp.float32))).astype(jnp.bfloat16)
        return grad_in, grad_wqkv, grad_wout, grad_wfc1, grad_wfc2

    return jax.shard_map(device_step, mesh=mesh, in_specs=in_specs, out_specs=out_specs, check_vma=False)
```

profile of v0, /device:TPU:21, one launch (start us, length us, event | category | flops | bytes accessed | tf_op | source)
XLA Modules:
  0.0 560.4 jit_solution(10240152118503002675)
XLA Ops:
  13.0 56.8 %all-gather.7.cloned.1.call-done = bf16[4096,1024]{1,0:T(8,128)(2,1)} async-done(((bf16[256,1024]{1,0:T(8,128)(2,1)}), bf16[4096,1024]{1,0:T(8,128)(2,1)}) %all-gather.7.cloned.1.call-update) | async-done | bytes 8388624 | tf_op jit(solution)/shard_map/all_gather | solution.py:66
  69.7 7.7 %fusion.78 = f32[4096,256]{1,0:T(8,128)} fusion(bf16[4096,1024]{1,0:T(8,128)(2,1)} %all-gather.7.cloned.1.call-done, bf16[1024,256]{1,0:T(8,128)(2,1)S(1)} %copy-done), kind=kOutput, calls=%fused_computation.96 | convolution fusion | flops 2147483648 | bytes 13107200 | tf_op jit(solution)/shard_map/dot_general | solution.py:68
  77.5 45.0 %all-gather.5.cloned.1.call-done = bf16[4096,1024]{1,0:T(8,128)(2,1)} async-done(((bf16[256,1024]{1,0:T(8,128)(2,1)}), bf16[4096,1024]{1,0:T(8,128)(2,1)}) %all-gather.5.cloned.1.call-update) | async-done | bytes 8388624 | tf_op jit(solution)/shard_map/all_gather | solution.py:67
  122.4 9.8 %fusion.7 = bf16[4096,256]{1,0:T(8,128)(2,1)S(1)} fusion(bf16[4096,1024]{1,0:T(8,128)(2,1)} %all-gather.5.cloned.1.call-done, bf16[256,1024]{1,0:T(8,128)(2,1)S(1)} %copy-done.34, f32[4096,256]{1,0:T(8,128)} %fusion.78), kind=kOutput, calls=%fused_computation.17 | convolution fusion | flops 2167406592 | bytes 15204352 | tf_op jit(solution)/shard_map/tm,fm->tf/dot_general | solution.py:72
  133.5 5.6 %convolution_convert_fusion.1 = bf16[4096,1024]{1,0:T(8,128)(2,1)} fusion(bf16[4096,256]{1,0:T(8,128)(2,1)S(1)} %fusion.7, bf16[1024,256]{1,0:T(8,128)(2,1)S(1)} %copy-done), kind=kOutput, calls=%fused_computation.13 | convolution fusion | flops 2151677952 | bytes 11010048 | tf_op jit(solution)/shard_map/tf,mf->tm/dot_general | solution.py:75
  141.1 61.0 %reduce-scatter.3.cloned.1.call-done = bf16[256,1024]{1,0:T(8,128)(2,1)} async-done(((bf16[4096,1024]{1,0:T(8,128)(2,1)}), bf16[256,1024]{1,0:T(8,128)(2,1)}) %reduce-scatter.3.cloned.1.call-update) | async-done | bytes 524304 | tf_op jit(solution)/shard_map/reduce_scatter | solution.py:76
  203.5 2.3 fusion.74
  206.5 52.2 %all-gather.9.cloned.1.call-done = bf16[4096,1024]{1,0:T(8,128)(2,1)} async-done(((bf16[256,1024]{1,0:T(8,128)(2,1)}), bf16[4096,1024]{1,0:T(8,128)(2,1)}) %all-gather.9.cloned.1.call-update) | async-done | bytes 8388624 | tf_op jit(solution)/shard_map/all_gather | solution.py:80
  258.7 6.3 %convolution_convert_fusion.2 = bf16[4096,192]{0,1:T(8,128)(2,1)S(1)} fusion(bf16[4096,1024]{1,0:T(8,128)(2,1)} %all-gather.9.cloned.1.call-done, bf16[1024,192]{0,1:T(8,128)(2,1)S(1)} %copy-done.15), kind=kOutput, calls=%fused_computation.18 | convolution fusion | flops 1611399168 | bytes 10354688 | tf_op jit(solution)/shard_map/dot_general | solution.py:37
  265.0 24.2 %fusion.2 = (f32[4096]{0:T(1024)S(1)}, f32[4096,4096]{0,1:T(8,128)}) fusion(bf16[4096,1,3,64]{0,3,2,1:T(8,128)(2,1)S(1)} %bitcast.82), kind=kOutput, calls=%fused_computation.7 | convolution fusion | flops 2214588416 | bytes 68173824 | tf_op jit(solution)/shard_map/qnd,knd->nqk/dot_general | solution.py:42
  289.3 21.8 %fusion.1 = f32[4096]{0:T(1024)S(1)} fusion(f32[4096,4096]{0,1:T(8,128)} %get-tuple-element.10, f32[4096]{0:T(1024)S(1)} %get-tuple-element.9), kind=kLoop, calls=%fused_computation.6 | loop fusion | flops 83881984 | bytes 67141632 | tf_op jit(solution)/shard_map/reduce_sum | solution.py:44
  311.9 6.0 %convolution_convert_fusion.4 = bf16[4096,64]{0,1:T(8,128)(2,1)S(1)} fusion(bf16[4096,1024]{1,0:T(8,128)(2,1)} %all-gather.11.cloned.1.call-done, bf16[1,64,1024]{2,1,0:T(8,128)(2,1)S(1)} %copy-done.17), kind=kOutput, calls=%fused_computation.20 | convolution fusion | flops 537133056 | bytes 9043968 | tf_op jit(solution)/shard_map/tm,ndm->tnd/dot_general | solution.py:47
  317.9 28.9 %fusion.18 = bf16[4096,1,1,64]{0,3,2,1:T(8,128)(2,1)} fusion(bf16[4096,64]{0,1:T(8,128)(2,1)S(1)} %convolution_convert_fusion.4, f32[4096,4096]{0,1:T(8,128)} %get-tuple-element.10, f32[4096]{0:T(1024)S(1)} %fusion.1, f32[4096]{0:T(1024)S(1)} %get-tuple-element.9), kind=kOutput, calls=%fused_computation.26 | convolution fusion | flops 2248409088 | bytes 68190208 | tf_op jit(solution)/shard_map/nqk,qnd->knd/dot_general | solution.py:48
  346.9 49.2 %multiply_reduce_fusion = (f32[4096]{0:T(1024)S(1)}, f32[4096,4096]{0,1:T(8,128)}) fusion(f32[4096]{0:T(1024)S(1)} %fusion.1, f32[4096]{0:T(1024)S(1)} %get-tuple-element.9, f32[4096,4096]{0,1:T(8,128)} %get-tuple-element.10, bf16[4096,64]{0,1:T(8,128)(2,1)S(1)} %convolution_convert_fusion.4, bf16[4096,1,3,64]{0,3,2,1:T(8,128)(2,1)S(1)} %bitcast.83), kind=kOutput, calls=%fused_computation.1 | convolution fusion | flops 2264920064 | bytes 135315456 | tf_op jit(solution)/shard_map/qnd,knd->nqk/dot_general | solution.py:49
  396.1 53.4 %multiply_convert_fusion = bf16[4096,4096]{0,1:T(8,128)(2,1)} fusion(f32[4096,4096]{0,1:T(8,128)} %get-tuple-element.12, f32[4096]{0:T(1024)S(1)} %get-tuple-element.11, f32[4096]{0:T(1024)S(1)} %fusion.1, f32[4096]{0:T(1024)S(1)} %get-tuple-element.9, f32[4096,4096]{0,1:T(8,128)} %get-tuple-element.10), kind=kLoop, calls=%fused_computation | loop fusion | flops 150994944 | bytes 167821312 | tf_op jit(solution)/shard_map/convert_element_type | solution.py:51
  449.5 15.5 %fusion.21 = bf16[4096,1,1,64]{0,3,2,1:T(8,128)(2,1)S(1)} fusion(bf16[4096,4096]{0,1:T(8,128)(2,1)} %multiply_convert_fusion, bf16[4096,1,3,64]{0,3,2,1:T(8,128)(2,1)S(1)} %bitcast.84), kind=kOutput, calls=%fused_computation.27 | convolution fusion | flops 2147745792 | bytes 34603008 | tf_op jit(solution)/shard_map/nqk,qnd->knd/dot_general | solution.py:53
  465.0 13.9 %fusion.14 = bf16[4096,1,1,64]{0,3,2,1:T(8,128)(2,1)S(1)} fusion(bf16[4096,4096]{0,1:T(8,128)(2,1)} %multiply_convert_fusion, bf16[4096,1,3,64]{0,3,2,1:T(8,128)(2,1)S(1)} %bitcast.85), kind=kOutput, calls=%fused_computation.24 | convolution fusion | flops 2147745792 | bytes 34603008 | tf_op jit(solution)/shard_map/nqk,knd->qnd/dot_general | solution.py:52
  480.3 5.6 %convolution_convert_fusion = bf16[4096,1024]{1,0:T(8,128)(2,1)} fusion(bf16[4096,192]{0,1:T(8,128)(2,1)S(1)} %bitcast.80, bf16[1024,192]{0,1:T(8,128)(2,1)S(1)} %copy-done.16), kind=kOutput, calls=%fused_computation.12 | convolution fusion | flops 1614807040 | bytes 10354688 | tf_op jit(solution)/shard_map/tc,mc->tm/dot_general | solution.py:85
  486.0 6.7 %convolution_convert_fusion.6 = bf16[1024,256]{1,0:T(8,128)(2,1)} fusion(bf16[4096,1024]{1,0:T(8,128)(2,1)} %all-gather.7.cloned.1.call-done, bf16[4096,256]{1,0:T(8,128)(2,1)S(1)} %copy-done.7), kind=kOutput, calls=%fused_computation.46 | convolution fusion | flops 2147745792 | bytes 11010048 | tf_op jit(solution)/shard_map/tm,tf->mf/dot_general | solution.py:74
  492.7 6.9 %fusion.35 = bf16[256,1024]{1,0:T(8,128)(2,1)} fusion(bf16[4096,1024]{1,0:T(8,128)(2,1)} %all-gather.5.cloned.1.call-done, f32[4096,256]{1,0:T(8,128)S(1)} %copy-done.35), kind=kOutput, calls=%fused_computation.45 | convolution fusion | flops 2157182976 | bytes 13107200 | tf_op jit(solution)/shard_map/tf,tm->fm/dot_general | solution.py:71
  499.6 2.5 convolution_convert_fusion.7
  502.3 30.8 %fusion.49 = bf16[1,64,1024]{2,1,0:T(8,128)(2,1)} fusion(bf16[4096,1024]{1,0:T(8,128)(2,1)} %all-gather.11.cloned.1.call-done, bf16[4096,1,3,64]{0,3,2,1:T(8,128)(2,1)} %bitcast.86, f32[4096,4096]{0,1:T(8,128)} %get-tuple-element.10, f32[4096]{0:T(1024)S(1)} %fusion.1, f32[4096]{0:T(1024)S(1)} %get-tuple-element.9), kind=kOutput, calls=%fused_computation.59 | convolution fusion | flops 2785345536 | bytes 76185600 | tf_op jit(solution)/shard_map/tnd,tm->ndm/dot_general | solution.py:83
  533.1 15.9 %reduce-scatter.5.cloned.1.call-done = bf16[256,1024]{1,0:T(8,128)(2,1)} async-done(((bf16[4096,1024]{1,0:T(8,128)(2,1)}), bf16[256,1024]{1,0:T(8,128)(2,1)}) %reduce-scatter.5.cloned.1.call-update) | async-done | bytes 524304 | tf_op jit(solution)/shard_map/reduce_scatter | solution.py:86
  550.5 2.6 fusion.57
  (106 shorter events, 14.6 us)
Async XLA Ops:
  7.2 62.6 %copy-start = (bf16[1024,256]{1,0:T(8,128)(2,1)S(1)}, bf16[1024,256]{1,0:T(8,128)(2,1)}, u32[]{:S(2)}) copy-start(bf16[1024,256]{1,0:T(8,128)(2,1)} %param.16) | copy-start | bytes 1572868
  7.2 62.5 %all-gather.7.cloned.1.call-start = ((), (), s32[]{:S(2)}) async-start(), calls=%async_computation.3 | async-start | bytes 8912896 | tf_op jit(solution)/shard_map/all_gather | solution.py:66
  8.5 195.0 %copy-start.22 = (f32[256]{0:T(256)}, f32[256]{0:T(256)S(1)}, u32[]{:S(2)}) copy-start(f32[256]{0:T(256)S(1)} %broadcast_multiply_fusion.5) | copy-start | bytes 3076
  9.9 193.7 %copy-start.24 = (f32[256]{0:T(256)}, f32[256]{0:T(256)S(1)}, u32[]{:S(2)}) copy-start(f32[256]{0:T(256)S(1)} %add_rsqrt_fusion.1) | copy-start | bytes 3076
  12.1 110.4 %all-gather.5.cloned.1.call-start = ((), (), s32[]{:S(2)}) async-start(), calls=%async_computation.2 | async-start | bytes 8912896 | tf_op jit(solution)/shard_map/all_gather | solution.py:67
  12.9 109.6 %copy-start.34 = (bf16[256,1024]{1,0:T(8,128)(2,1)S(1)}, bf16[256,1024]{1,0:T(8,128)(2,1)}, u32[]{:S(2)}) copy-start(bf16[256,1024]{1,0:T(8,128)(2,1)} %param.17) | copy-start | bytes 1572868
  12.9 189.2 %reduce-scatter.3.cloned.1.call-start = ((), (), s32[]{:S(2)}) async-start(), calls=%async_computation.4 | async-start | bytes 8912896 | tf_op jit(solution)/shard_map/reduce_scatter | solution.py:76
  139.2 62.9 %copy-start.2 = (bf16[256,1024]{1,0:T(8,128)(2,1)S(1)}, bf16[256,1024]{1,0:T(8,128)(2,1)}, u32[]{:S(2)}) copy-start(bf16[256,1024]{1,0:T(8,128)(2,1)} %param.10) | copy-start | bytes 1572868
  139.2 62.9 %copy-start.18 = (f32[1024]{0:T(1024)S(1)}, f32[1024]{0:T(1024)}, u32[]{:S(2)}) copy-start(f32[1024]{0:T(1024)} %param.13) | copy-start | bytes 12292
  139.2 64.4 %copy-start.10 = (bf16[256,1024]{1,0:T(8,128)(2,1)S(1)}, bf16[256,1024]{1,0:T(8,128)(2,1)}, u32[]{:S(2)}) copy-start(bf16[256,1024]{1,0:T(8,128)(2,1)} %param.11) | copy-start | bytes 1572868
  139.2 119.6 %copy-start.15 = (bf16[1024,192]{0,1:T(8,128)(2,1)S(1)}, bf16[1024,192]{0,1:T(8,128)(2,1)}, u32[]{:S(2)}) copy-start(bf16[1024,192]{0,1:T(8,128)(2,1)} %param.14) | copy-start | bytes 1179652
  139.2 119.5 %all-gather.9.cloned.1.call-start = ((), (), s32[]{:S(2)}) async-start(), calls=%async_computation.5 | async-start | bytes 8912896 | tf_op jit(solution)/shard_map/all_gather | solution.py:80
  139.5 67.0 %copy-start.26 = (f32[256]{0:T(256)}, f32[256]{0:T(256)S(1)}, u32[]{:S(2)}) copy-start(f32[256]{0:T(256)S(1)} %broadcast_multiply_fusion.2) | copy-start | bytes 3076
  139.8 66.6 %copy-start.28 = (f32[256]{0:T(256)}, f32[256]{0:T(256)S(1)}, u32[]{:S(2)}) copy-start(f32[256]{0:T(256)S(1)} %add_rsqrt_fusion) | copy-start | bytes 3076
  141.0 170.9 %all-gather.11.cloned.1.call-start = ((), (), s32[]{:S(2)}) async-start(), calls=%async_computation.6 | async-start | bytes 8912896 | tf_op jit(solution)/shard_map/all_gather | solution.py:81
  205.9 343.0 %reduce-scatter.5.cloned.1.call-start = ((), (), s32[]{:S(2)}) async-start(), calls=%async_computation.7 | async-start | bytes 8912896 | tf_op jit(solution)/shard_map/reduce_scatter | solution.py:86
  265.0 200.0 %copy-start.13 = (bf16[4096,192]{0,1:T(8,128)(2,1)}, bf16[4096,192]{0,1:T(8,128)(2,1)S(1)}, u32[]{:S(2)}) copy-start(bf16[4096,192]{0,1:T(8,128)(2,1)S(1)} %convolution_convert_fusion.2) | copy-start | bytes 4718596
  502.2 48.2 %copy-start.3 = (bf16[256,1024]{1,0:T(8,128)(2,1)S(1)}, bf16[256,1024]{1,0:T(8,128)(2,1)}, u32[]{:S(2)}) copy-start(bf16[256,1024]{1,0:T(8,128)(2,1)} %param.10) | copy-start | bytes 1572868
  502.2 48.2 %copy-start.11 = (bf16[256,1024]{1,0:T(8,128)(2,1)S(1)}, bf16[256,1024]{1,0:T(8,128)(2,1)}, u32[]{:S(2)}) copy-start(bf16[256,1024]{1,0:T(8,128)(2,1)} %param.11) | copy-start | bytes 1572868
  502.2 48.2 %copy-start.12 = (bf16[256,1024]{1,0:T(8,128)(2,1)S(1)}, bf16[256,1024]{1,0:T(8,128)(2,1)}, u32[]{:S(2)}) copy-start(bf16[256,1024]{1,0:T(8,128)(2,1)} %reduce-scatter.3.cloned.1.call-done) | copy-start | bytes 1572868
  502.2 48.2 %copy-start.19 = (f32[1024]{0:T(1024)S(1)}, f32[1024]{0:T(1024)}, u32[]{:S(2)}) copy-start(f32[1024]{0:T(1024)} %param.13) | copy-start | bytes 12292
  502.2 48.2 %copy-start.23 = (f32[256]{0:T(256)S(1)}, f32[256]{0:T(256)}, u32[]{:S(2)}) copy-start(f32[256]{0:T(256)} %copy-done.22) | copy-start | bytes 3076
  502.2 48.2 %copy-start.25 = (f32[256]{0:T(256)S(1)}, f32[256]{0:T(256)}, u32[]{:S(2)}) copy-start(f32[256]{0:T(256)} %copy-done.24) | copy-start | bytes 3076
  502.3 50.9 %copy-start.1 = (bf16[1024,256]{1,0:T(8,128)(2,1)S(1)}, bf16[1024,256]{1,0:T(8,128)(2,1)}, u32[]{:S(2)}) copy-start(bf16[1024,256]{1,0:T(8,128)(2,1)} %param.16) | copy-start | bytes 1572868
  (20 other events, 390.0 us)
Sparse Core Ops, SparseCore 0:
  12.2 57.5 all-gather.6
  71.4 51.0 all-gather.4
  139.4 62.6 reduce-scatter.2
  204.1 54.5 all-gather.8
  260.8 51.0 all-gather.10
  486.1 62.7 reduce-scatter.4
where the time goes:
time: 571 us; the launch traced here: 560 us
  waiting for transfers between devices  233 us (41%)
  matrix products  220 us (39%)
  other arithmetic  89.4 us (16%)
  between operations  15 us (3%)
    reduce_scatter x1, waiting for transfers between devices, device_step(): lax.psum_scatter(norm2_part, 'tp', scatter_dimension=0, tiled=True)  61 us
    all_gather x1, waiting for transfers between devices, device_step(): ln2_all = lax.all_gather(ln2_loc, 'tp', axis=0, tiled=True)  56.8 us
    convert_element_type x1, other arithmetic, attention_grads(): (attn_prob * (grad_prob - row_dot) * score_scale).astype(jnp.bfloat16)  53.4 us
    all_gather x1, waiting for transfers between devices, device_step(): ln1_all = lax.all_gather(ln1_loc, 'tp', axis=0, tiled=True)  52.2 us
    dot_general x1, matrix products, attention_grads(): jnp.einsum('qnd,knd->nqk', grad_attn, v_rows, preferred_element_type=jnp....  49.2 us
    all_gather x1, waiting for transfers between devices, device_step(): gout_all = lax.all_gather(gout_rows, 'tp', axis=0, tiled=True)  45 us
    dot_general x1, matrix products, device_step(): jnp.einsum('tnd,tm->ndm', attn_out, grad_mid_all, preferred_element_type=...  30.8 us
    dot_general x1, matrix products, attention_grads(): jnp.einsum('nqk,qnd->knd', prob_low, grad_attn, preferred_element_type=jn...  28.9 us
  transfers between devices with their start and end apart: 6, of which 6 were waited for; matrix products, arithmetic and copies ran while one was open for 20% of the time, Pallas kernels for 0%

commit v1 on v0

v1 whole, which is shorter than its diff:
```python
import functools

import jax
import jax.numpy as jnp
from jax import lax
from jax.experimental import pallas as pl
from jax.experimental.pallas import tpu as pltpu
from jax.sharding import PartitionSpec as P

LN_EPS = 1e-5
GELU_COEF = 0.044715
GELU_SCALE = 0.7978845608028654
QB = 256
TK = 512
NEG = -1e30
F32 = jnp.float32
BF16 = jnp.bfloat16


def ln_forward(rows):
    row_mean = jnp.mean(rows, axis=-1, keepdims=True)
    centered = rows - row_mean
    row_rstd = lax.rsqrt(jnp.mean(centered * centered, axis=-1, keepdims=True) + LN_EPS)
    return centered * row_rstd, row_rstd


def ln_backward(x_hat, row_rstd, ln_gain, grad_norm):
    grad_hat = grad_norm * ln_gain
    proj_one = jnp.mean(grad_hat, axis=-1, keepdims=True)
    proj_two = jnp.mean(grad_hat * x_hat, axis=-1, keepdims=True)
    return row_rstd * (grad_hat - proj_one - x_hat * proj_two)


def gelu_pair(pre_act):
    tanh_val = jnp.tanh(GELU_SCALE * (pre_act + GELU_COEF * pre_act * pre_act * pre_act))
    gelu_val = 0.5 * pre_act * (1.0 + tanh_val)
    gelu_der = 0.5 * (1.0 + tanh_val) + 0.5 * pre_act * (1.0 - tanh_val * tanh_val) * GELU_SCALE * (1.0 + 3.0 * GELU_COEF * pre_act * pre_act)
    return gelu_val, gelu_der


def dot_nt(a, b):
    return lax.dot_general(a, b, (((1,), (1,)), ((), ())), preferred_element_type=F32)


def dot_nn(a, b):
    return lax.dot_general(a, b, (((1,), (0,)), ((), ())), preferred_element_type=F32)


def keep_mask(first_key, first_query):
    key = first_key + lax.broadcasted_iota(jnp.int32, (TK, QB), 0)
    query = first_query + lax.broadcasted_iota(jnp.int32, (TK, QB), 1)
    return key <= query


def fwd_block(i, q_ref, kv_ref, kvt_ref, ot_ref, lse_ref, head):
    rows = pl.ds(pl.multiple_of(i * QB, QB), QB)
    queries = q_ref[rows, :]

    def tile(t, carry, masked):
        top, total, acc = carry
        keys = pl.ds(pl.multiple_of(t * TK, TK), TK)
        s = dot_nt(kv_ref[keys, :], queries)
        if masked:
            s = jnp.where(keep_mask(t * TK, i * QB), s, NEG)
        new_top = jnp.maximum(top, jnp.max(s, axis=0, keepdims=True))
        p = jnp.exp(s - new_top)
        scale = jnp.exp(top - new_top)
        total = total * scale + jnp.sum(p, axis=0, keepdims=True)
        acc = acc * scale + dot_nn(kvt_ref[head:, keys], p.astype(BF16))
        return new_top, total, acc

    init = (jnp.full((1, QB), NEG, F32), jnp.zeros((1, QB), F32), jnp.zeros((head, QB), F32))
    last = lax.div(i, TK // QB)
    carry = lax.fori_loop(0, last, lambda t, c: tile(t, c, False), init)
    top, total, acc = tile(last, carry, True)
    ot_ref[:, rows] = acc / total
    lse_ref[:, rows] = top + jnp.log(total)


def bwd_block(i, q_ref, do_ref, kv_ref, kvt_ref, ot_ref, lse_ref, dq_ref, dkv_ref, head):
    rows = pl.ds(pl.multiple_of(i * QB, QB), QB)
    grads = do_ref[rows, :]
    both = jnp.concatenate([q_ref[rows, :], grads], axis=0)
    lse = lse_ref[:, rows]
    grads_t = jnp.transpose(grads.astype(F32))[head:]
    row_dot = jnp.sum(grads_t * ot_ref[:, rows], axis=0, keepdims=True)

    def tile(t, dqt, masked):
        keys = pl.ds(pl.multiple_of(t * TK, TK), TK)
        sr = dot_nt(kv_ref[keys, :], both)
        p = jnp.exp(sr[:, :QB] - lse)
        if masked:
            p = jnp.where(keep_mask(t * TK, i * QB), p, 0.0)
        ds = (p * (sr[:, QB:] - row_dot)).astype(BF16)
        dkv_ref[keys, :] += dot_nn(jnp.concatenate([ds, p.astype(BF16)], axis=1), both)
        return dqt + dot_nn(kvt_ref[:head, keys], ds)

    last = lax.div(i, TK // QB)
    dqt = lax.fori_loop(0, last, lambda t, c: tile(t, c, False), jnp.zeros((head, QB), F32))
    dqt = tile(last, dqt, True) * (head ** -0.5)
    dqt = jnp.concatenate([dqt, jnp.zeros_like(dqt)], axis=0)
    dq_ref[rows, :] = jnp.transpose(dqt).astype(BF16)


def attention_forward(q_pad, kv, kvt):
    tokens, wide = q_pad.shape
    head = wide // 2

    def kernel(q_ref, kv_ref, kvt_ref, ot_ref, lse_ref):
        def step(i, _):
            fwd_block(i, q_ref, kv_ref, kvt_ref, ot_ref, lse_ref, head)
            return 0
        lax.fori_loop(0, tokens // QB, step, 0)

    flops = 2 * tokens * tokens * wide
    return pl.pallas_call(
        kernel,
        out_shape=(jax.ShapeDtypeStruct((head, tokens), F32), jax.ShapeDtypeStruct((1, tokens), F32)),
        compiler_params=pltpu.CompilerParams(vmem_limit_bytes=48 * 1024 * 1024),
        cost_estimate=pl.CostEstimate(flops=8 * flops, bytes_accessed=4 * tokens * wide, transcendentals=tokens * tokens // 2),
    )(q_pad, kv, kvt)


def attention_backward(q_pad, do_pad, kv, kvt, out_t, lse):
    tokens, wide = q_pad.shape
    head = wide // 2

    def kernel(q_ref, do_ref, kv_ref, kvt_ref, ot_ref, lse_ref, dq_ref, dkv_ref, acc_ref):
        acc_ref[...] = jnp.zeros_like(acc_ref)

        def step(i, _):
            bwd_block(i, q_ref, do_ref, kv_ref, kvt_ref, ot_ref, lse_ref, dq_ref, acc_ref, head)
            return 0
        lax.fori_loop(0, tokens // QB, step, 0)
        dkv_ref[...] = acc_ref[...].astype(BF16)

    flops = 4 * tokens * tokens * wide
    return pl.pallas_call(
        kernel,
        out_shape=(jax.ShapeDtypeStruct((tokens, wide), BF16), jax.ShapeDtypeStruct((tokens, wide), BF16)),
        scratch_shapes=[pltpu.VMEM((tokens, wide), F32)],
        compiler_params=pltpu.CompilerParams(vmem_limit_bytes=48 * 1024 * 1024),
        cost_estimate=pl.CostEstimate(flops=8 * flops, bytes_accessed=6 * tokens * wide, transcendentals=tokens * tokens // 2),
    )(q_pad, do_pad, kv, kvt, out_t, lse)


def solution(mesh):
    row_spec = P(('dp', 'tp'), None)
    in_specs = (row_spec, row_spec, row_spec, P(None), P(None), P(None, 'tp'), P('tp', None, None), P(None, 'tp'), P('tp', None))
    out_specs = (row_spec, P('dp', 'tp'), P(('dp', 'tp'), None, None), P('dp', 'tp'), P(('dp', 'tp'), None))

    def device_step(in_rows, mid_rows, gout_rows, ln1_gain, ln2_gain, wqkv_loc, wout_loc, wfc1_loc, wfc2_loc):
        head, width = wout_loc.shape[1:]
        wqkv_pad = jnp.concatenate([wqkv_loc[:, :head], jnp.zeros_like(wqkv_loc[:, :head]), wqkv_loc[:, head:]], axis=1)
        wout_pad = jnp.concatenate([jnp.zeros_like(wout_loc[0]), wout_loc[0]], axis=0)
        mid_hat, mid_rstd = ln_forward(mid_rows.astype(F32))
        ln2_loc = (mid_hat * ln2_gain).astype(BF16)
        ln2_all = lax.all_gather(ln2_loc, 'tp', axis=0, tiled=True)
        gout_all = lax.all_gather(gout_rows, 'tp', axis=0, tiled=True)
        in_hat, in_rstd = ln_forward(in_rows.astype(F32))
        ln1_loc = (in_hat * ln1_gain).astype(BF16)
        ln1_all = lax.all_gather(ln1_loc, 'tp', axis=0, tiled=True)
        pre_act = jnp.dot(ln2_all, wfc1_loc, preferred_element_type=F32)
        gelu_val, gelu_der = gelu_pair(pre_act)
        act_low = gelu_val.astype(BF16)
        grad_wfc2 = jnp.einsum('tf,tm->fm', act_low, gout_all, preferred_element_type=F32).astype(BF16)
        grad_act = jnp.einsum('tm,fm->tf', gout_all, wfc2_loc, preferred_element_type=F32)
        grad_pre = (grad_act * gelu_der).astype(BF16)
        grad_wfc1 = jnp.einsum('tm,tf->mf', ln2_all, grad_pre, preferred_element_type=F32).astype(BF16)
        norm2_part = jnp.einsum('tf,mf->tm', grad_pre, wfc1_loc, preferred_element_type=F32).astype(BF16)
        grad_norm2 = lax.psum_scatter(norm2_part, 'tp', scatter_dimension=0, tiled=True)
        grad_mid = gout_rows.astype(F32) + ln_backward(mid_hat, mid_rstd, ln2_gain, grad_norm2.astype(F32))
        qkv_pad = jnp.dot(ln1_all, wqkv_pad, preferred_element_type=F32).astype(BF16)
        q_pad = qkv_pad[:, :2 * head] * jnp.asarray(head ** -0.5, BF16)
        kv = qkv_pad[:, 2 * head:]
        kvt = kv.T
        out_t, lse = attention_forward(q_pad, kv, kvt)
        grad_mid_all = lax.all_gather(grad_mid.astype(BF16), 'tp', axis=0, tiled=True)
        do_pad = jnp.einsum('tm,dm->td', grad_mid_all, wout_pad, preferred_element_type=F32).astype(BF16)
        dq_pad, dkv = attention_backward(q_pad, do_pad, kv, kvt, out_t, lse)
        grad_wout = jnp.dot(out_t.astype(BF16), grad_mid_all, preferred_element_type=F32).astype(BF16)[None]
        grad_qkv = jnp.concatenate([dq_pad, dkv], axis=1)
        grad_wqkv = jnp.einsum('tm,tc->mc', ln1_all, grad_qkv, preferred_element_type=F32).astype(BF16)
        grad_wqkv = jnp.concatenate([grad_wqkv[:, :head], grad_wqkv[:, 2 * head:]], axis=1)
        norm1_part = jnp.einsum('tc,mc->tm', grad_qkv, wqkv_pad, preferred_element_type=F32).astype(BF16)
        grad_norm1 = lax.psum_scatter(norm1_part, 'tp', scatter_dimension=0, tiled=True)
        grad_in = (grad_mid + ln_backward(in_hat, in_rstd, ln1_gain, grad_norm1.astype(F32))).astype(BF16)
        return grad_in, grad_wqkv, grad_wout, grad_wfc1, grad_wfc2

    return jax.shard_map(device_step, mesh=mesh, in_specs=in_specs, out_specs=out_specs, check_vma=False)
```

time: 571 us -> 440 us (0.77); the launches traced: 560 us -> 438 us
  matrix products: 220 us -> 59.7 us
  Pallas kernels: 0 us -> 76.5 us
  other arithmetic: 89.4 us -> 16 us
  waiting for transfers between devices: 233 us -> 261 us
  local copies, waits for them, and re-layouts: 2.71 us -> 9.94 us
    dot_general x15 -> x10, matrix products: 220 us -> 59.7 us  [the longest x1 9.78 us: device_step(): jnp.einsum('tm,fm->tf', gout_all, wfc2_loc, preferred_element_type=F32)]
    pallas_call x0 -> x2, Pallas kernels: none -> 76.5 us  [the longest x1 38.7 us: attention_backward(): pl.pallas_call(kernel, out_shape=(jax.ShapeDtypeStruct((tokens, wide), BF...]
    convert_element_type x5 -> x4, other arithmetic: 61.6 us -> 8.18 us  [the longest x1 2.64 us: device_step(): (grad_mid + ln_backward(in_hat, in_rstd, ln1_gain, grad_norm1.astype(F32)...]
    reduce_scatter x1, waiting for transfers between devices: 15.9 us -> 41 us  [device_step(): lax.psum_scatter(norm1_part, 'tp', scatter_dimension=0, tiled=True)]
    reduce_sum x1 -> x0, other arithmetic: 21.8 us -> none  [attention_grads(): attn_prob = jax.nn.softmax(jnp.where(causal, scores, -1e+30), axis=-1)]
  transfers between devices with their start and end apart: 6 -> 6, of which waited for: 6 -> 6; matrix products, arithmetic and copies ran while one was open for 20% -> 10% of each run, Pallas kernels for 0% -> 9%
where the time goes in v1:
time: 440 us; the launch traced here: 438 us
  waiting for transfers between devices  261 us (59%)
  Pallas kernels  76.5 us (17%)
  matrix products  59.7 us (14%)
  other arithmetic  16 us (4%)
  between operations  14.6 us (3%)
  local copies, waits for them, and re-layouts  9.94 us (2%)
    reduce_scatter x1, waiting for transfers between devices, device_step(): lax.psum_scatter(norm2_part, 'tp', scatter_dimension=0, tiled=True)  59.3 us
    all_gather x1, waiting for transfers between devices, device_step(): ln2_all = lax.all_gather(ln2_loc, 'tp', axis=0, tiled=True)  56.8 us
    all_gather x1, waiting for transfers between devices, device_step(): ln1_all = lax.all_gather(ln1_loc, 'tp', axis=0, tiled=True)  52.4 us
    all_gather x1, waiting for transfers between devices, device_step(): gout_all = lax.all_gather(gout_rows, 'tp', axis=0, tiled=True)  45 us
    reduce_scatter x1, waiting for transfers between devices, device_step(): lax.psum_scatter(norm1_part, 'tp', scatter_dimension=0, tiled=True)  41 us
    pallas_call x1, Pallas kernels, attention_backward(): pl.pallas_call(kernel, out_shape=(jax.ShapeDtypeStruct((tokens, wide), BF...  38.7 us
    pallas_call x1, Pallas kernels, attention_forward(): pl.pallas_call(kernel, out_shape=(jax.ShapeDtypeStruct((head, tokens), F3...  37.8 us
    dot_general x1, matrix products, device_step(): jnp.einsum('tm,fm->tf', gout_all, wfc2_loc, preferred_element_type=F32)  9.78 us
  transfers between devices with their start and end apart: 6, of which 6 were waited for; matrix products, arithmetic and copies ran while one was open for 10% of the time, Pallas kernels for 9%

profile of v1, /device:TPU:21, one launch (start us, length us, event | category | flops | bytes accessed | tf_op | source)
XLA Modules:
  0.0 437.9 jit_solution(11610673942662523849)
XLA Ops:
  9.9 2.1 fusion.30
  13.0 56.8 %all-gather.7.cloned.1.call-done = bf16[4096,1024]{1,0:T(8,128)(2,1)} async-done(((bf16[256,1024]{1,0:T(8,128)(2,1)}), bf16[4096,1024]{1,0:T(8,128)(2,1)}) %all-gather.7.cloned.1.call-update) | async-done | bytes 8388624 | tf_op jit(solution)/shard_map/all_gather | solution.py:158
  69.7 7.7 %fusion.50 = f32[4096,256]{1,0:T(8,128)} fusion(bf16[4096,1024]{1,0:T(8,128)(2,1)} %all-gather.7.cloned.1.call-done, bf16[1024,256]{1,0:T(8,128)(2,1)S(1)} %copy-done), kind=kOutput, calls=%fused_computation.81 | convolution fusion | flops 2147483648 | bytes 13107200 | tf_op jit(solution)/shard_map/dot_general | solution.py:163
  77.4 45.0 %all-gather.5.cloned.1.call-done = bf16[4096,1024]{1,0:T(8,128)(2,1)} async-done(((bf16[256,1024]{1,0:T(8,128)(2,1)}), bf16[4096,1024]{1,0:T(8,128)(2,1)}) %all-gather.5.cloned.1.call-update) | async-done | bytes 8388624 | tf_op jit(solution)/shard_map/all_gather | solution.py:159
  122.4 9.8 %fusion = bf16[4096,256]{1,0:T(8,128)(2,1)S(1)} fusion(bf16[4096,1024]{1,0:T(8,128)(2,1)} %all-gather.5.cloned.1.call-done, bf16[256,1024]{1,0:T(8,128)(2,1)S(1)} %copy-done.35, f32[4096,256]{1,0:T(8,128)} %fusion.50), kind=kOutput, calls=%fused_computation.5 | convolution fusion | flops 2167406592 | bytes 15204352 | tf_op jit(solution)/shard_map/tm,fm->tf/dot_general | solution.py:167
  133.6 5.6 %convolution_convert_fusion.1 = bf16[4096,1024]{1,0:T(8,128)(2,1)} fusion(bf16[4096,256]{1,0:T(8,128)(2,1)S(1)} %fusion, bf16[1024,256]{1,0:T(8,128)(2,1)S(1)} %copy-done), kind=kOutput, calls=%fused_computation.1 | convolution fusion | flops 2151677952 | bytes 11010048 | tf_op jit(solution)/shard_map/tf,mf->tm/dot_general | solution.py:170
  142.8 59.3 %reduce-scatter.3.cloned.1.call-done = bf16[256,1024]{1,0:T(8,128)(2,1)} async-done(((bf16[4096,1024]{1,0:T(8,128)(2,1)}), bf16[256,1024]{1,0:T(8,128)(2,1)}) %reduce-scatter.3.cloned.1.call-update) | async-done | bytes 524304 | tf_op jit(solution)/shard_map/reduce_scatter | solution.py:171
  203.6 2.3 fusion.49
  206.3 52.4 %all-gather.9.cloned.1.call-done = bf16[4096,1024]{1,0:T(8,128)(2,1)} async-done(((bf16[256,1024]{1,0:T(8,128)(2,1)}), bf16[4096,1024]{1,0:T(8,128)(2,1)}) %all-gather.9.cloned.1.call-update) | async-done | bytes 8388624 | tf_op jit(solution)/shard_map/all_gather | solution.py:162
  258.8 5.8 %convolution_convert_fusion.2 = bf16[4096,256]{0,1:T(8,128)(2,1)S(1)} fusion(bf16[4096,1024]{1,0:T(8,128)(2,1)} %all-gather.9.cloned.1.call-done, bf16[1024,128]{0,1:T(8,128)(2,1)S(1)} %slice.19, bf16[1024,64]{0,1:T(8,128)(2,1)S(1)} %slice.18, bf16[256]{0:T(256)(128)(2,1)S(1)} %pad.4.clone), kind=kOutput, calls=%fused_computation.6 | convolution fusion | flops 2150105088 | bytes 10879488 | tf_op jit(solution)/shard_map/dot_general | solution.py:173
  266.4 1.6 copy.17.q_ref
  268.0 37.8 %shard_map.128 = (f32[64,4096]{1,0:T(8,128)S(1)}, f32[1,4096]{1,0:T(1,128)S(1)}) custom-call(bf16[4096,128]{1,0:T(8,128)(2,1)S(1)} %copy.17.q_ref, bf16[4096,128]{1,0:T(8,128)(2,1)S(1)} %copy.18.kv_ref, bf16[128,4096]{1,0:T(8,128)(2,1)S(1)} %get-tuple-element.17.kvt_ref), custom_call_target="tpu_custom_call" | custom-call | flops 34359738368 | bytes 2097152 | tf_op jit(solution)/shard_map/pallas_call | solution.py:116
  306.8 5.1 %all-gather.11.cloned.1.call-done = bf16[4096,1024]{1,0:T(8,128)(2,1)} async-done(((bf16[256,1024]{1,0:T(8,128)(2,1)}), bf16[4096,1024]{1,0:T(8,128)(2,1)}) %all-gather.11.cloned.1.call-update) | async-done | bytes 8388624 | tf_op jit(solution)/shard_map/all_gather | solution.py:178
  312.0 5.7 %convolution_convert_fusion.3.do_ref = bf16[4096,128]{1,0:T(8,128)(2,1)S(1)} fusion(bf16[4096,1024]{1,0:T(8,128)(2,1)} %all-gather.11.cloned.1.call-done, bf16[64,1024]{1,0:T(8,128)(2,1)} %bitcast.24), kind=kOutput, calls=%fused_computation.7 | convolution fusion | flops 1074266112 | bytes 9568256 | tf_op jit(solution)/shard_map/tm,dm->td/dot_general | solution.py:179
  317.7 38.7 %shard_map.129 = (bf16[4096,128]{1,0:T(8,128)(2,1)S(1)}, bf16[4096,128]{1,0:T(8,128)(2,1)S(1)}) custom-call(bf16[4096,128]{1,0:T(8,128)(2,1)S(1)} %copy.17.q_ref, bf16[4096,128]{1,0:T(8,128)(2,1)S(1)} %convolution_convert_fusion.3.do_ref, bf16[4096,128]{1,0:T(8,128)(2,1)S(1)} %copy.18.kv_ref, bf16[128,4096]{1,0:T(8,128)(2,1)} %copy-done.4, ...), custom_call_target="tpu_custom_call" | custom-call | flops 68719476736 | bytes 3145728 | tf_op jit(solution)/shard_map/pallas_call | solution.py:138
  358.2 5.7 %convolution_convert_fusion = bf16[4096,1024]{1,0:T(8,128)(2,1)} fusion(bf16[4096,256]{1,0:T(8,128)(2,1)S(1)} %constant_dynamic-update-slice_fusion, bf16[1024,128]{0,1:T(8,128)(2,1)S(1)} %slice.19, bf16[1024,64]{0,1:T(8,128)(2,1)S(1)} %slice.18, bf16[256]{0:T(256)(128)(2,1)S(1)} %copy-done.34), kind=kOutput, calls=%fused_computation | convolution fusion | flops 2153250816 | bytes 10879488 | tf_op jit(solution)/shard_map/tc,mc->tm/dot_general | solution.py:185
  364.0 1.5 copy-done.10
  365.5 6.7 %convolution_convert_fusion.4 = bf16[1024,256]{1,0:T(8,128)(2,1)} fusion(bf16[4096,1024]{1,0:T(8,128)(2,1)} %all-gather.7.cloned.1.call-done, bf16[4096,256]{1,0:T(8,128)(2,1)S(1)} %copy-done.10), kind=kOutput, calls=%fused_computation.24 | convolution fusion | flops 2147745792 | bytes 11010048 | tf_op jit(solution)/shard_map/tm,tf->mf/dot_general | solution.py:169
  372.2 8.1 %fusion.11 = bf16[256,1024]{1,0:T(8,128)(2,1)} fusion(bf16[4096,1024]{1,0:T(8,128)(2,1)} %all-gather.5.cloned.1.call-done, f32[4096,256]{1,0:T(8,128)} %fusion.50), kind=kOutput, calls=%fused_computation.23 | convolution fusion | flops 2157182976 | bytes 13107200 | tf_op jit(solution)/shard_map/tf,tm->fm/dot_general | solution.py:166
  380.4 2.4 convolution_convert_fusion.5
  383.7 2.2 fusion.22
  386.0 41.0 %reduce-scatter.5.cloned.1.call-done = bf16[256,1024]{1,0:T(8,128)(2,1)} async-done(((bf16[4096,1024]{1,0:T(8,128)(2,1)}), bf16[256,1024]{1,0:T(8,128)(2,1)}) %reduce-scatter.5.cloned.1.call-update) | async-done | bytes 524304 | tf_op jit(solution)/shard_map/reduce_scatter | solution.py:186
  426.9 1.4 fusion.36
  428.4 2.6 fusion.28
  (117 shorter events, 15.8 us)
Async XLA Ops:
  7.2 62.6 %copy-start = (bf16[1024,256]{1,0:T(8,128)(2,1)S(1)}, bf16[1024,256]{1,0:T(8,128)(2,1)}, u32[]{:S(2)}) copy-start(bf16[1024,256]{1,0:T(8,128)(2,1)} %param.16) | copy-start | bytes 1572868
  7.2 62.5 %all-gather.7.cloned.1.call-start = ((), (), s32[]{:S(2)}) async-start(), calls=%async_computation.3 | async-start | bytes 8912896 | tf_op jit(solution)/shard_map/all_gather | solution.py:158
  8.5 195.0 %copy-start.21 = (f32[256]{0:T(256)}, f32[256]{0:T(256)S(1)}, u32[]{:S(2)}) copy-start(f32[256]{0:T(256)S(1)} %broadcast_multiply_fusion.5) | copy-start | bytes 3076
  9.9 193.7 %copy-start.23 = (f32[256]{0:T(256)}, f32[256]{0:T(256)S(1)}, u32[]{:S(2)}) copy-start(f32[256]{0:T(256)S(1)} %add_rsqrt_fusion.1) | copy-start | bytes 3076
  12.1 110.4 %all-gather.5.cloned.1.call-start = ((), (), s32[]{:S(2)}) async-start(), calls=%async_computation.2 | async-start | bytes 8912896 | tf_op jit(solution)/shard_map/all_gather | solution.py:159
  12.9 109.6 %copy-start.35 = (bf16[256,1024]{1,0:T(8,128)(2,1)S(1)}, bf16[256,1024]{1,0:T(8,128)(2,1)}, u32[]{:S(2)}) copy-start(bf16[256,1024]{1,0:T(8,128)(2,1)} %param.17) | copy-start | bytes 1572868
  12.9 189.2 %reduce-scatter.3.cloned.1.call-start = ((), (), s32[]{:S(2)}) async-start(), calls=%async_computation.4 | async-start | bytes 8912896 | tf_op jit(solution)/shard_map/reduce_scatter | solution.py:171
  139.2 62.9 %copy-start.5 = (bf16[256,1024]{1,0:T(8,128)(2,1)S(1)}, bf16[256,1024]{1,0:T(8,128)(2,1)}, u32[]{:S(2)}) copy-start(bf16[256,1024]{1,0:T(8,128)(2,1)} %param.10) | copy-start | bytes 1572868
  139.2 62.9 %copy-start.17 = (f32[1024]{0:T(1024)S(1)}, f32[1024]{0:T(1024)}, u32[]{:S(2)}) copy-start(f32[1024]{0:T(1024)} %param.13) | copy-start | bytes 12292
  139.2 64.4 %copy-start.13 = (bf16[256,1024]{1,0:T(8,128)(2,1)S(1)}, bf16[256,1024]{1,0:T(8,128)(2,1)}, u32[]{:S(2)}) copy-start(bf16[256,1024]{1,0:T(8,128)(2,1)} %param.11) | copy-start | bytes 1572868
  139.3 66.9 %copy-start.16 = (bf16[1024,192]{0,1:T(8,128)(2,1)S(1)}, bf16[1024,192]{0,1:T(8,128)(2,1)}, u32[]{:S(2)}) copy-start(bf16[1024,192]{0,1:T(8,128)(2,1)} %param.14) | copy-start | bytes 1179652
  139.3 119.5 %all-gather.9.cloned.1.call-start = ((), (), s32[]{:S(2)}) async-start(), calls=%async_computation.5 | async-start | bytes 8912896 | tf_op jit(solution)/shard_map/all_gather | solution.py:162
  142.7 169.3 %all-gather.11.cloned.1.call-start = ((), (), s32[]{:S(2)}) async-start(), calls=%async_computation.6 | async-start | bytes 8912896 | tf_op jit(solution)/shard_map/all_gather | solution.py:178
  203.5 55.2 %copy-start.31 = (f32[256]{0:T(256)}, f32[256]{0:T(256)S(1)}, u32[]{:S(2)}) copy-start(f32[256]{0:T(256)S(1)} %get-tuple-element.21) | copy-start | bytes 3076
  203.5 61.0 %copy-start.29 = (f32[256]{0:T(256)}, f32[256]{0:T(256)S(1)}, u32[]{:S(2)}) copy-start(f32[256]{0:T(256)S(1)} %get-tuple-element.20) | copy-start | bytes 3076
  205.9 221.0 %reduce-scatter.5.cloned.1.call-start = ((), (), s32[]{:S(2)}) async-start(), calls=%async_computation.7 | async-start | bytes 8912896 | tf_op jit(solution)/shard_map/reduce_scatter | solution.py:186
  206.3 52.4 %copy-start.33 = (bf16[256]{0:T(256)(128)(2,1)}, bf16[256]{0:T(256)(128)(2,1)S(1)}, u32[]{:S(2)}) copy-start(bf16[256]{0:T(256)(128)(2,1)S(1)} %pad.4.clone) | copy-start | bytes 1540
  383.6 44.7 %copy-start.6 = (bf16[256,1024]{1,0:T(8,128)(2,1)S(1)}, bf16[256,1024]{1,0:T(8,128)(2,1)}, u32[]{:S(2)}) copy-start(bf16[256,1024]{1,0:T(8,128)(2,1)} %param.10) | copy-start | bytes 1572868
  383.6 44.7 %copy-start.14 = (bf16[256,1024]{1,0:T(8,128)(2,1)S(1)}, bf16[256,1024]{1,0:T(8,128)(2,1)}, u32[]{:S(2)}) copy-start(bf16[256,1024]{1,0:T(8,128)(2,1)} %param.11) | copy-start | bytes 1572868
  383.7 44.7 %copy-start.15 = (bf16[256,1024]{1,0:T(8,128)(2,1)S(1)}, bf16[256,1024]{1,0:T(8,128)(2,1)}, u32[]{:S(2)}) copy-start(bf16[256,1024]{1,0:T(8,128)(2,1)} %reduce-scatter.3.cloned.1.call-done) | copy-start | bytes 1572868
  383.7 44.7 %copy-start.18 = (f32[1024]{0:T(1024)S(1)}, f32[1024]{0:T(1024)}, u32[]{:S(2)}) copy-start(f32[1024]{0:T(1024)} %param.13) | copy-start | bytes 12292
  383.7 44.7 %copy-start.22 = (f32[256]{0:T(256)S(1)}, f32[256]{0:T(256)}, u32[]{:S(2)}) copy-start(f32[256]{0:T(256)} %copy-done.21) | copy-start | bytes 3076
  383.7 44.7 %copy-start.24 = (f32[256]{0:T(256)S(1)}, f32[256]{0:T(256)}, u32[]{:S(2)}) copy-start(f32[256]{0:T(256)} %copy-done.23) | copy-start | bytes 3076
  383.7 47.4 %copy-start.1 = (bf16[1024,256]{1,0:T(8,128)(2,1)S(1)}, bf16[1024,256]{1,0:T(8,128)(2,1)}, u32[]{:S(2)}) copy-start(bf16[1024,256]{1,0:T(8,128)(2,1)} %param.16) | copy-start | bytes 1572868
  (22 other events, 378.2 us)
Sparse Core Ops, SparseCore 0:
  12.2 57.5 all-gather.6
  71.4 51.0 all-gather.4
  139.4 62.6 reduce-scatter.2
  204.1 54.5 all-gather.8
  260.8 51.0 all-gather.10
  364.1 62.7 reduce-scatter.4

commit v2 on v0

v2 whole, which is shorter than its diff:
```python
import jax
import jax.numpy as jnp
from jax import lax
from jax.experimental import pallas as pl
from jax.experimental.pallas import tpu as pltpu
from jax.sharding import PartitionSpec as P

LN_EPS = 1e-5
GELU_COEF = 0.044715
GELU_SCALE = 0.7978845608028654
NEG = -1e30
F32 = jnp.float32
BF16 = jnp.bfloat16
MESH = pl.DeviceIdType.MESH
SIGN = (1, -1)
N2, DY, N1, EG = 0, 1, 2, 3


def ln_forward(rows):
    row_mean = jnp.mean(rows, axis=-1, keepdims=True)
    centered = rows - row_mean
    row_rstd = lax.rsqrt(jnp.mean(centered * centered, axis=-1, keepdims=True) + LN_EPS)
    return centered * row_rstd, row_rstd


def ln_backward(x_hat, row_rstd, ln_gain, grad_norm):
    grad_hat = grad_norm * ln_gain
    proj_one = jnp.mean(grad_hat, axis=-1, keepdims=True)
    proj_two = jnp.mean(grad_hat * x_hat, axis=-1, keepdims=True)
    return row_rstd * (grad_hat - proj_one - x_hat * proj_two)


def gelu_pair(pre_act):
    tanh_val = jnp.tanh(GELU_SCALE * (pre_act + GELU_COEF * pre_act * pre_act * pre_act))
    gelu_val = 0.5 * pre_act * (1.0 + tanh_val)
    gelu_der = 0.5 * (1.0 + tanh_val) + 0.5 * pre_act * (1.0 - tanh_val * tanh_val) * GELU_SCALE * (1.0 + 3.0 * GELU_COEF * pre_act * pre_act)
    return gelu_val, gelu_der


def dot_nt(a, b):
    return lax.dot_general(a, b, (((1,), (1,)), ((), ())), preferred_element_type=F32)


def dot_nn(a, b):
    return lax.dot_general(a, b, (((1,), (0,)), ((), ())), preferred_element_type=F32)


def ds_of(index, size):
    return pl.ds(pl.multiple_of(index * size, size), size)


def keep_mask(first_key, first_query, shape):
    key = first_key + lax.broadcasted_iota(jnp.int32, shape, 0)
    query = first_query + lax.broadcasted_iota(jnp.int32, shape, 1)
    return key <= query


def layer_kernel(chips, x_ref, h_ref, g_ref, gain1_ref, gain2_ref, wqkv_ref, wo_ref, w1_ref, w2_ref,
                 dx_ref, dwqkv_ref, dwo_ref, dw1_ref, dw2_ref,
                 n2_all, dy_all, n1_all, part, dbuf, rbuf, q_all, do_all, kv_all, kvt_all, ot_all, lse_all,
                 dq_all, dkv_acc, dw1t_acc, dw2_acc, dwo_acc, dwqkvt_acc, dh1,
                 ag_send, ag_recv, dd_send, dd_recv, rs_send, rs_recv, dx_send, dx_recv):
    me = lax.axis_index('tp')
    z, c = lax.div(me, 2), lax.rem(me, 2)
    half_ring = chips // 2
    last_u = 2 * half_ring
    R, width = x_ref.shape
    H = R // 2
    head = dwo_ref.shape[1]
    blocks = 2 * chips
    keys_per = 2 * R
    full = (n2_all, dy_all, n1_all, dy_all)

    def chip_at(offset):
        return lax.rem(z + offset + 2 * chips, chips)

    nbr = tuple(2 * chip_at(s) + c for s in SIGN)
    partner = 2 * z + 1 - c

    def half_rows(chip, core, h):
        return ds_of(2 * (2 * chip + core) + h, H)

    def block_rows(block):
        return ds_of(block, R)

    def ag_copy(a, d, s, h, src=None):
        dst = full[a].at[half_rows(chip_at(-SIGN[d] * (s - 1)), c, h)]
        return pltpu.make_async_remote_copy(dst if src is None else src, dst, ag_send.at[a, d, s - 1, h],
                                            ag_recv.at[a, d, s - 1, h], device_id={'tp': nbr[d]}, device_id_type=MESH)

    def ag_arrived(a, d, s, h):
        dst = full[a].at[half_rows(chip_at(-SIGN[d] * s), c, h)]
        pltpu.make_async_remote_copy(dst, dst, ag_send.at[a, d, s - 1, h],
                                     ag_recv.at[a, d, s - 1, h], device_id={'tp': nbr[d]}, device_id_type=MESH).wait_recv()

    def dd_copy(a, j, chip, core, h, src=None):
        dst = full[a].at[half_rows(chip, core, h)]
        return pltpu.make_async_remote_copy(dst if src is None else src, dst, dd_send.at[a, j, h], dd_recv.at[a, j, h],
                                            device_id={'tp': partner}, device_id_type=MESH)

    def slot_of(step, d):
        return jnp.where(step == 0, 0, jnp.minimum(2 * step - 1 + d, chips - 1))

    def chip_of_slot(j):
        away = lax.div(j + 1, 2)
        return chip_at(jnp.where(lax.rem(j, 2) == 1, -away, away))

    def dx_copy(r, j):
        chip = chip_of_slot(j)
        return pltpu.make_async_remote_copy(part.at[block_rows(2 * chip + 1 - c)], dbuf.at[chip], dx_send.at[r, j],
                                            dx_recv.at[r, j], device_id={'tp': partner}, device_id_type=MESH)

    def rs_copy(r, d, s, h):
        src = part.at[half_rows(chip_at(SIGN[d] * (half_ring - s + 1)), c, h)]
        return pltpu.make_async_remote_copy(src, rbuf.at[d, s - 1, h], rs_send.at[r, d, s - 1, h],
                                            rs_recv.at[r, d, s - 1, h], device_id={'tp': nbr[d]}, device_id_type=MESH)

    def ag_begin(a, src=None):
        for h in (0, 1):
            part_src = None if src is None else src.at[pl.ds(h * H, H)]
            for d in (0, 1):
                ag_copy(a, d, 1, h, part_src).start()
            dd_copy(a, 0, z, c, h, part_src).start()

    def ag_sent(a):
        for h in (0, 1):
            for d in (0, 1):
                for s in range(1, half_ring + 1):
                    if s < half_ring or h == d:
                        ag_copy(a, d, s, h).wait_send()
            for j in range(chips):
                dd_copy(a, j, chip_of_slot(j), c, h).wait_send()

    def ag_loop(arrays, before, compute, after):
        def body(u, carry):
            step, h = lax.div(u, 2), lax.rem(u, 2)
            s = step + 1

            @pl.when(u < last_u)
            def _():
                for a in arrays:
                    for d in (0, 1):
                        @pl.when((s < half_ring) | (h == d))
                        def _():
                            ag_arrived(a, d, s, h)

                            @pl.when((s < half_ring - 1) | ((s == half_ring - 1) & (h == d)))
                            def _():
                                ag_copy(a, d, s + 1, h).start()
                            dd_copy(a, slot_of(s, d), chip_at(-SIGN[d] * s), c, h).start()
            before(u)

            def one(sub, carry):
                chip = chip_at((2 * sub - 1) * step)
                core = jnp.where(h == 0, c, 1 - c)

                @pl.when(h == 1)
                def _():
                    for a in arrays:
                        for g in (0, 1):
                            dd_copy(a, slot_of(step, sub), chip, 1 - c, g).wait_recv()
                compute(2 * chip + core)
                return carry
            lax.fori_loop(0, jnp.where((step == 0) | (step == half_ring), 1, 2), one, 0)
            after(u)
            return carry
        lax.fori_loop(0, last_u + 2, body, 0)

    def rs_begin(r):
        for d in (0, 1):
            rs_copy(r, d, 1, d).start()
            rs_copy(r, d, 2, 1 - d).start()

    def rs_tick(r, u):
        s = 1 + lax.div(u, 2)
        odd = lax.rem(u, 2)
        for d in (0, 1):
            h = jnp.where(odd == 1, d, 1 - d)
            rs_copy(r, d, s, h).wait_recv()
            rows = half_rows(chip_at(SIGN[d] * (half_ring - s)), c, h)
            part[rows, :] = (part[rows, :].astype(F32) + rbuf[d, s - 1, h].astype(F32)).astype(BF16)
        for d in (0, 1):
            rs_copy(r, d, s + 1, jnp.where(odd == 1, d, 1 - d)).start()

    def rs_last(r, h):
        for d in (0, 1):
            rs_copy(r, d, half_ring, h).wait_recv()
        own = part[half_rows(z, c, h), :].astype(F32)
        return own + rbuf[0, half_ring - 1, h].astype(F32) + rbuf[1, half_ring - 1, h].astype(F32)

    def rs_sent(r):
        for d in (0, 1):
            for h in (0, 1):
                for s in range(1, half_ring + 1):
                    if s > 1 or h == d:
                        rs_copy(r, d, s, h).wait_send()
        for j in range(chips):
            dx_copy(r, j).wait_send()

    def join_partner(r, j):
        dx_copy(r, j).wait_recv()
        chip = chip_of_slot(j)
        rows = block_rows(2 * chip + c)
        part[rows, :] = (part[rows, :].astype(F32) + dbuf[chip].astype(F32)).astype(BF16)

    def mlp(block):
        rows = block_rows(block)
        n2, dy = n2_all[rows, :], dy_all[rows, :]
        gelu_val, gelu_der = gelu_pair(dot_nn(n2, w1_ref[...]))
        grad_pre = dot_nt(dy, w2_ref[...]) * gelu_der
        dw2_acc[...] += dot_nn(jnp.transpose(gelu_val).astype(BF16), dy)
        dw1t_acc[...] += dot_nn(jnp.transpose(grad_pre).astype(BF16), n2)
        part[rows, :] = dot_nt(grad_pre.astype(BF16), w1_ref[...]).astype(BF16)

    def qkv(block):
        rows = block_rows(block)
        cols = dot_nn(n1_all[rows, :], wqkv_ref[...])
        q_all[rows, :] = cols[:, :2 * head].astype(BF16) * jnp.asarray(head ** -0.5, BF16)
        kv_all[rows, :] = cols[:, 2 * head:].astype(BF16)
        kvt_all[:, rows] = jnp.transpose(cols[:, 2 * head:]).astype(BF16)

    def attend(i):
        rows = block_rows(i)
        queries = q_all[rows, :]

        def tile(t, carry, masked):
            top, total, acc = carry
            keys = ds_of(t, keys_per)
            s = dot_nt(kv_all[keys, :], queries)
            if masked:
                s = jnp.where(keep_mask(t * keys_per, i * R, s.shape), s, NEG)
            new_top = jnp.maximum(top, jnp.max(s, axis=0, keepdims=True))
            p = jnp.exp(s - new_top)
            scale = jnp.exp(top - new_top)
            total = total * scale + jnp.sum(p, axis=0, keepdims=True)
            acc = acc * scale + dot_nn(kvt_all[head:, keys], p.astype(BF16))
            return new_top, total, acc

        init = (jnp.full((1, R), NEG, F32), jnp.zeros((1, R), F32), jnp.zeros((head, R), F32))
        last = lax.div(i, 2)
        top, total, acc = tile(last, lax.fori_loop(0, last, lambda t, k: tile(t, k, False), init), True)
        ot_all[:, rows] = acc / total
        lse_all[:, rows] = top + jnp.log(total)

    def attend_grad(i):
        rows = block_rows(i)
        e_rows = dy_all[rows, :]
        grads_wide = dot_nt(e_rows, wo_ref[...])
        grads = grads_wide.astype(BF16)
        grads_t = jnp.transpose(grads.astype(F32))[head:]
        out_t = ot_all[:, rows]
        dwo_acc[...] += dot_nn(out_t.astype(BF16), e_rows)
        row_dot = jnp.sum(grads_t * out_t, axis=0, keepdims=True)
        both = jnp.concatenate([q_all[rows, :], grads], axis=0)
        lse = lse_all[:, rows]

        def tile(t, dqt, masked):
            keys = ds_of(t, keys_per)
            sr = dot_nt(kv_all[keys, :], both)
            p = jnp.exp(sr[:, :R] - lse)
            if masked:
                p = jnp.where(keep_mask(t * keys_per, i * R, p.shape), p, 0.0)
            ds = (p * (sr[:, R:] - row_dot)).astype(BF16)
            dkv_acc[keys, :] += dot_nn(jnp.concatenate([ds, p.astype(BF16)], axis=1), both)
            return dqt + dot_nn(kvt_all[:head, keys], ds)

        last = lax.div(i, 2)
        dqt = lax.fori_loop(0, last, lambda t, k: tile(t, k, False), jnp.zeros((head, R), F32))
        dqt = tile(last, dqt, True) * (head ** -0.5)
        dq_all[rows, :] = jnp.transpose(jnp.concatenate([dqt, jnp.zeros_like(dqt)], axis=0)).astype(BF16)

    def grad_cols(block):
        rows = block_rows(block)
        return jnp.concatenate([dq_all[rows, :], dkv_acc[rows, :].astype(BF16)], axis=1)

    def nothing(u):
        del u

    barrier = pltpu.get_barrier_semaphore()
    for peer in nbr + (partner,):
        pl.semaphore_signal(barrier, inc=1, device_id={'tp': peer}, device_id_type=MESH)
    pl.semaphore_wait(barrier, 3)
    ag_begin(DY, g_ref)

    def norm_rows(k, carry):
        piece = H // 2
        src = ds_of(k, piece)
        dst = ds_of((2 * z + c) * 4 + k, piece)
        for raw, gain, out in ((h_ref, gain2_ref, n2_all), (x_ref, gain1_ref, n1_all)):
            out[dst, :] = (ln_forward(raw[src, :].astype(F32))[0] * gain[...]).astype(BF16)
        dy_all[dst, :] = g_ref[src, :]
        return carry
    lax.fori_loop(0, 4, norm_rows, 0)
    for acc in (dw1t_acc, dw2_acc):
        acc[...] = jnp.zeros_like(acc)
    ag_begin(N2)
    for acc in (dwo_acc, dwqkvt_acc, dkv_acc):
        acc[...] = jnp.zeros_like(acc)

    def send_partner(u):
        step = lax.div(u, 2)

        @pl.when((lax.rem(u, 2) == 0) & (u > 0))
        def _():
            dx_copy(0, slot_of(step - 1, 0)).start()

            @pl.when(step > 1)
            def _():
                dx_copy(0, slot_of(step - 1, 1)).start()

    def begin_n1(u):
        @pl.when(u == last_u - 3)
        def _():
            ag_begin(N1)

    ag_loop((DY, N2), send_partner, mlp, begin_n1)

    dx_pending = slot_of(half_ring, 0)

    def join_first(u):
        @pl.when(u == 0)
        def _():
            dx_copy(0, dx_pending).start()

        @pl.when((u > 0) & (u <= chips))
        def _():
            join_partner(0, chips - u)

    def begin_rs(u):
        @pl.when(u == last_u - 2)
        def _():
            ag_sent(N2)
            ag_sent(DY)
            rs_begin(0)

    ag_loop((N1,), join_first, qkv, begin_rs)

    def forward_pair(u, carry):
        @pl.when(u <= last_u - 3)
        def _():
            rs_tick(0, u)

        def one(k, carry):
            attend(jnp.where(k == 0, blocks - u, u - 1))
            return carry
        return lax.fori_loop(0, 2, one, carry)
    lax.fori_loop(1, chips + 1, forward_pair, 0)

    for h in (0, 1):
        rows = pl.ds(h * H, H)
        mid_hat, mid_rstd = ln_forward(h_ref[rows, :].astype(F32))
        grad = g_ref[rows, :].astype(F32) + ln_backward(mid_hat, mid_rstd, gain2_ref[...], rs_last(0, h))
        dh1[rows, :] = grad
        dy_all[half_rows(z, c, h), :] = grad.astype(BF16)
    rs_sent(0)
    ag_begin(EG)

    ag_loop((EG,), nothing, attend_grad, nothing)

    def share(k, carry):
        j = chips - 1 - k
        chip = chip_of_slot(j)
        for core in (1 - c, c):
            block = 2 * chip + core
            part[block_rows(block), :] = dot_nt(grad_cols(block), wqkv_ref[...]).astype(BF16)
        dx_copy(1, j).start()

        @pl.when(k > 0)
        def _():
            join_partner(1, j + 1)

        @pl.when(k == 3)
        def _():
            rs_begin(1)
        return carry
    lax.fori_loop(0, chips, share, 0)
    join_partner(1, 0)

    def weight_block(u, carry):
        @pl.when(u <= last_u - 3)
        def _():
            rs_tick(1, u)
        block = u - 1
        cols_t = jnp.transpose(grad_cols(block).astype(F32)).astype(BF16)
        dwqkvt_acc[...] += dot_nn(cols_t, n1_all[block_rows(block), :])
        return carry
    lax.fori_loop(1, blocks + 1, weight_block, 0)

    dw2_ref[...] = dw2_acc[...].astype(BF16)
    dw1_ref[...] = jnp.transpose(dw1t_acc[...]).astype(BF16)
    dwo_ref[0] = dwo_acc[...].astype(BF16)
    dwqkv_t = jnp.concatenate([dwqkvt_acc[:head, :], dwqkvt_acc[2 * head:, :], jnp.zeros((head, width), F32)], axis=0)
    dwqkv_ref[...] = jnp.transpose(dwqkv_t)[:, :3 * head].astype(BF16)

    for h in (0, 1):
        rows = pl.ds(h * H, H)
        in_hat, in_rstd = ln_forward(x_ref[rows, :].astype(F32))
        dx_ref[rows, :] = (dh1[rows, :] + ln_backward(in_hat, in_rstd, gain1_ref[...], rs_last(1, h))).astype(BF16)
    rs_sent(1)
    ag_sent(N1)
    ag_sent(EG)


def solution(mesh):
    chips = mesh.shape['tp'] // 2
    row_spec = P(('dp', 'tp'), None)
    in_specs = (row_spec, row_spec, row_spec, P(None), P(None), P(None, 'tp'), P('tp', None, None), P(None, 'tp'), P('tp', None))
    out_specs = (row_spec, P('dp', 'tp'), P(('dp', 'tp'), None, None), P('dp', 'tp'), P(('dp', 'tp'), None))

    def device_step(in_rows, mid_rows, gout_rows, ln1_gain, ln2_gain, wqkv_loc, wout_loc, wfc1_loc, wfc2_loc):
        R, width = in_rows.shape
        head = wout_loc.shape[1]
        hidden = wfc1_loc.shape[1]
        tokens = 2 * chips * R
        half_ring = chips // 2
        wqkv_pad = jnp.concatenate([wqkv_loc[:, :head], jnp.zeros_like(wqkv_loc[:, :head]), wqkv_loc[:, head:]], axis=1)
        wout_pad = jnp.concatenate([jnp.zeros_like(wout_loc[0]), wout_loc[0]], axis=0)
        vm = pltpu.VMEM
        dma = pltpu.SemaphoreType.DMA
        scratch = [
            vm((tokens, width), BF16), vm((tokens, width), BF16), vm((tokens, width), BF16), vm((tokens, width), BF16),
            vm((chips, R, width), BF16), vm((2, half_ring, 2, R // 2, width), BF16),
            vm((tokens, 2 * head), BF16), vm((8, 128), BF16), vm((tokens, 2 * head), BF16), vm((2 * head, tokens), BF16),
            vm((head, tokens), F32), vm((1, tokens), F32),
            vm((tokens, 2 * head), BF16), vm((tokens, 2 * head), F32),
            vm((hidden, width), F32), vm((hidden, width), F32), vm((head, width), F32), vm((4 * head, width), F32), vm((R, width), F32),
            dma((4, 2, half_ring, 2)), dma((4, 2, half_ring, 2)), dma((4, chips, 2)), dma((4, chips, 2)),
            dma((2, 2, half_ring, 2)), dma((2, 2, half_ring, 2)), dma((2, chips)), dma((2, chips)),
        ]
        return pl.pallas_call(
            lambda *refs: layer_kernel(chips, *refs),
            out_shape=(
                jax.ShapeDtypeStruct((R, width), BF16), jax.ShapeDtypeStruct((width, 3 * head), BF16),
                jax.ShapeDtypeStruct((1, head, width), BF16), jax.ShapeDtypeStruct((width, hidden), BF16),
                jax.ShapeDtypeStruct((hidden, width), BF16)),
            in_specs=[pl.BlockSpec(memory_space=pltpu.VMEM)] * 9,
            out_specs=tuple([pl.BlockSpec(memory_space=pltpu.VMEM)] * 5),
            scratch_shapes=scratch,
            compiler_params=pltpu.CompilerParams(collective_id=0, has_side_effects=True, vmem_limit_bytes=67043328),
        )(in_rows, mid_rows, gout_rows, ln1_gain[None], ln2_gain[None], wqkv_pad, wout_pad, wfc1_loc, wfc2_loc)

    return jax.shard_map(device_step, mesh=mesh, in_specs=in_specs, out_specs=out_specs, check_vma=False)
```

time: 571 us -> 306 us (0.54); the launches traced: 560 us -> 305 us
  Pallas kernels: 0 us -> 294 us
  waiting for transfers between devices: 233 us -> 0 us
  matrix products: 220 us -> 0 us
  other arithmetic: 89.4 us -> 0.91 us
  between operations: 15 us -> 0.68 us
  local copies, waits for them, and re-layouts: 2.71 us -> 9.44 us
    pallas_call x0 -> x1, Pallas kernels: none -> 294 us  [device_step(): pl.pallas_call(lambda *refs: layer_kernel(chips, *refs), out_shape=(jax.S...]
    dot_general x15 -> x0, matrix products: 220 us -> none  [the longest x1 49.2 us: attention_grads(): jnp.einsum('qnd,knd->nqk', grad_attn, v_rows, preferred_element_type=jnp....]
    all_gather x4 -> x0, waiting for transfers between devices: 155 us -> none  [the longest x1 56.8 us: device_step(): ln2_all = lax.all_gather(ln2_loc, 'tp', axis=0, tiled=True)]
    reduce_scatter x2 -> x0, waiting for transfers between devices: 76.9 us -> none  [the longest x1 61 us: device_step(): lax.psum_scatter(norm2_part, 'tp', scatter_dimension=0, tiled=True)]
    convert_element_type x5 -> x0, other arithmetic: 61.6 us -> none  [the longest x1 53.4 us: attention_grads(): (attn_prob * (grad_prob - row_dot) * score_scale).astype(jnp.bfloat16)]
    reduce_sum x7 -> x0, other arithmetic: 27.6 us -> none  [the longest x1 21.8 us: attention_grads(): attn_prob = jax.nn.softmax(jnp.where(causal, scores, -1e+30), axis=-1)]
  transfers between devices with their start and end apart: 6 -> 0, of which waited for: 6 -> 0; matrix products, arithmetic and copies ran while one was open for 20% -> 0% of each run, Pallas kernels for 0% -> 0%
where the time goes in v2:
time: 306 us; the launch traced here: 305 us
  Pallas kernels  294 us (96%)
  local copies, waits for them, and re-layouts  9.44 us (3%)
    pallas_call x1, Pallas kernels, device_step(): pl.pallas_call(lambda *refs: layer_kernel(chips, *refs), out_shape=(jax.S...  294 us

profile of v2, /device:TPU:21, one launch (start us, length us, event | category | flops | bytes accessed | tf_op | source)
XLA Modules:
  0.0 305.2 jit_solution(13587008287580339262)
XLA Ops:
  0.6 0.1 pad.2.clone
  0.7 0.0 slice-start
  0.7 0.9 slice-done
  1.6 0.0 copy-start.3
  1.6 0.2 copy.17
  1.8 0.7 copy-done.3
  2.5 0.7 concatenate.7.refs_6_
  3.3 0.9 slice-done.1
  4.2 0.2 copy.18
  4.4 0.9 pad_maximum_fusion.refs_5_
  5.3 294.2 %shard_map.128 = (bf16[256,1024]{1,0:T(8,128)(2,1)}, bf16[1024,192]{1,0:T(8,128)(2,1)}, bf16[1,64,1024]{2,1,0:T(8,128)(2,1)}, bf16[1024,256]{1,0:T(8,128)(2,1)}, bf16[256,1024]{1,0:T(8,128)(2,1)}) custom-call(bf16[256,1024]{1,0:T(8,128)(2,1)} %refs_0_.1, bf16[256,1024]{1,0:T(8,128)(2,1)} %refs_1_.1, bf16[256,1024]{1,0:T(8,128)(2,1)} %refs_2_.1, ...), custom_call_target="tpu_custom_call" | custom-call | tf_op jit(solution)/shard_map/pallas_call | solution.py:430
  299.5 0.0 copy-start.2
  299.5 2.0 copy.16
  301.6 0.0 copy-done.2
  301.6 0.0 copy-start.4
  301.6 0.0 copy-start.1
  301.6 0.8 copy.23
  302.4 0.2 copy-done.4
  302.6 0.7 copy.24
  303.2 0.0 copy-done.1
  303.2 0.0 copy-start
  303.2 0.8 copy.25
  304.0 0.4 copy-done
  304.5 0.8 copy.26
  (2 shorter events, 0.0 us)
Async XLA Ops:
  0.7 0.9 slice-start
  1.6 0.9 copy-start.3
  3.2 0.9 slice-start.1
  299.5 2.0 copy-start.2
  301.6 1.0 copy-start.4
  301.6 1.7 copy-start.1
  303.2 1.2 copy-start

commit v3 on v2

--- a/solution.py
+++ b/solution.py
@@ -49,15 +49,13 @@
     return pl.ds(pl.multiple_of(index * size, size), size)
 
 
-def keep_mask(first_key, first_query, shape):
-    key = first_key + lax.broadcasted_iota(jnp.int32, shape, 0)
-    query = first_query + lax.broadcasted_iota(jnp.int32, shape, 1)
-    return key <= query
-
-
-def layer_kernel(chips, x_ref, h_ref, g_ref, gain1_ref, gain2_ref, wqkv_ref, wo_ref, w1_ref, w2_ref,
-                 dx_ref, dwqkv_ref, dwo_ref, dw1_ref, dw2_ref,
-                 n2_all, dy_all, n1_all, part, dbuf, rbuf, q_all, do_all, kv_all, kvt_all, ot_all, lse_all,
+def keep_mask(shape):
+    return lax.broadcasted_iota(jnp.int32, shape, 0) <= lax.broadcasted_iota(jnp.int32, shape, 1)
+
+
+def layer_kernel(chips, x_ref, h_ref, g_ref, gain1_ref, gain2_ref, wqkvt_ref, wo_ref, w1_ref, w2_ref,
+                 dx_ref, dwqkvt_ref, dwo_ref, dw1_ref, dw2_ref,
+                 n2_all, dy_all, n1_all, part, dbuf, rbuf, q_all, wot_pad, wqkvt_pad, kv_all, kvt_all, ot_all, lse_all,
                  dq_all, dkv_acc, dw1t_acc, dw2_acc, dwo_acc, dwqkvt_acc, dh1,
                  ag_send, ag_recv, dd_send, dd_recv, rs_send, rs_recv, dx_send, dx_recv):
     me = lax.axis_index('tp')
@@ -67,8 +65,7 @@
     R, width = x_ref.shape
     H = R // 2
     head = dwo_ref.shape[1]
-    blocks = 2 * chips
-    keys_per = 2 * R
+    pair = 2 * R
     full = (n2_all, dy_all, n1_all, dy_all)
 
     def chip_at(offset):
@@ -150,21 +147,16 @@
                             dd_copy(a, slot_of(s, d), chip_at(-SIGN[d] * s), c, h).start()
             before(u)
 
-            def one(sub, carry):
-                chip = chip_at((2 * sub - 1) * step)
-                core = jnp.where(h == 0, c, 1 - c)
-
-                @pl.when(h == 1)
-                def _():
-                    for a in arrays:
-                        for g in (0, 1):
-                            dd_copy(a, slot_of(step, sub), chip, 1 - c, g).wait_recv()
-                compute(2 * chip + core)
-                return carry
-            lax.fori_loop(0, jnp.where((step == 0) | (step == half_ring), 1, 2), one, 0)
+            @pl.when((h == 0) | ((step > 0) & (step < half_ring)))
+            def _():
+                chip = chip_at((2 * h - 1) * step)
+                for a in arrays:
+                    for g in (0, 1):
+                        dd_copy(a, slot_of(step, h), chip, 1 - c, g).wait_recv()
+                compute(chip)
             after(u)
             return carry
-        lax.fori_loop(0, last_u + 2, body, 0)
+        lax.fori_loop(0, last_u + 1, body, 0)
 
     def rs_begin(r):
         for d in (0, 1):
@@ -203,8 +195,8 @@
         rows = block_rows(2 * chip + c)
         part[rows, :] = (part[rows, :].astype(F32) + dbuf[chip].astype(F32)).astype(BF16)
 
-    def mlp(block):
-        rows = block_rows(block)
+    def mlp(chip):
+        rows = ds_of(chip, pair)
         n2, dy = n2_all[rows, :], dy_all[rows, :]
         gelu_val, gelu_der = gelu_pair(dot_nn(n2, w1_ref[...]))
         grad_pre = dot_nt(dy, w2_ref[...]) * gelu_der
@@ -212,23 +204,23 @@
         dw1t_acc[...] += dot_nn(jnp.transpose(grad_pre).astype(BF16), n2)
         part[rows, :] = dot_nt(grad_pre.astype(BF16), w1_ref[...]).astype(BF16)
 
-    def qkv(block):
-        rows = block_rows(block)
-        cols = dot_nn(n1_all[rows, :], wqkv_ref[...])
+    def qkv(chip):
+        rows = ds_of(chip, pair)
+        cols = dot_nt(n1_all[rows, :], wqkvt_pad[...])
         q_all[rows, :] = cols[:, :2 * head].astype(BF16) * jnp.asarray(head ** -0.5, BF16)
         kv_all[rows, :] = cols[:, 2 * head:].astype(BF16)
         kvt_all[:, rows] = jnp.transpose(cols[:, 2 * head:]).astype(BF16)
 
-    def attend(i):
-        rows = block_rows(i)
+    def attend(m):
+        rows = ds_of(m, pair)
         queries = q_all[rows, :]
 
         def tile(t, carry, masked):
             top, total, acc = carry
-            keys = ds_of(t, keys_per)
+            keys = ds_of(t, pair)
             s = dot_nt(kv_all[keys, :], queries)
             if masked:
-                s = jnp.where(keep_mask(t * keys_per, i * R, s.shape), s, NEG)
+                s = jnp.where(keep_mask(s.shape), s, NEG)
             new_top = jnp.maximum(top, jnp.max(s, axis=0, keepdims=True))
             p = jnp.exp(s - new_top)
             scale = jnp.exp(top - new_top)
@@ -236,17 +228,15 @@
             acc = acc * scale + dot_nn(kvt_all[head:, keys], p.astype(BF16))
             return new_top, total, acc
 
-        init = (jnp.full((1, R), NEG, F32), jnp.zeros((1, R), F32), jnp.zeros((head, R), F32))
-        last = lax.div(i, 2)
-        top, total, acc = tile(last, lax.fori_loop(0, last, lambda t, k: tile(t, k, False), init), True)
+        init = (jnp.full((1, pair), NEG, F32), jnp.zeros((1, pair), F32), jnp.zeros((head, pair), F32))
+        top, total, acc = tile(m, lax.fori_loop(0, m, lambda t, k: tile(t, k, False), init), True)
         ot_all[:, rows] = acc / total
         lse_all[:, rows] = top + jnp.log(total)
 
-    def attend_grad(i):
-        rows = block_rows(i)
+    def attend_grad(m):
+        rows = ds_of(m, pair)
         e_rows = dy_all[rows, :]
-        grads_wide = dot_nt(e_rows, wo_ref[...])
-        grads = grads_wide.astype(BF16)
+        grads = dot_nt(e_rows, wot_pad[...]).astype(BF16)
         grads_t = jnp.transpose(grads.astype(F32))[head:]
         out_t = ot_all[:, rows]
         dwo_acc[...] += dot_nn(out_t.astype(BF16), e_rows)
@@ -255,22 +245,20 @@
         lse = lse_all[:, rows]
 
         def tile(t, dqt, masked):
-            keys = ds_of(t, keys_per)
+            keys = ds_of(t, pair)
             sr = dot_nt(kv_all[keys, :], both)
-            p = jnp.exp(sr[:, :R] - lse)
+            p = jnp.exp(sr[:, :pair] - lse)
             if masked:
-                p = jnp.where(keep_mask(t * keys_per, i * R, p.shape), p, 0.0)
-            ds = (p * (sr[:, R:] - row_dot)).astype(BF16)
+                p = jnp.where(keep_mask(p.shape), p, 0.0)
+            ds = (p * (sr[:, pair:] - row_dot)).astype(BF16)
             dkv_acc[keys, :] += dot_nn(jnp.concatenate([ds, p.astype(BF16)], axis=1), both)
             return dqt + dot_nn(kvt_all[:head, keys], ds)
 
-        last = lax.div(i, 2)
-        dqt = lax.fori_loop(0, last, lambda t, k: tile(t, k, False), jnp.zeros((head, R), F32))
-        dqt = tile(last, dqt, True) * (head ** -0.5)
+        dqt = lax.fori_loop(0, m, lambda t, k: tile(t, k, False), jnp.zeros((head, pair), F32))
+        dqt = tile(m, dqt, True) * (head ** -0.5)
         dq_all[rows, :] = jnp.transpose(jnp.concatenate([dqt, jnp.zeros_like(dqt)], axis=0)).astype(BF16)
 
-    def grad_cols(block):
-        rows = block_rows(block)
+    def grad_cols(rows):
         return jnp.concatenate([dq_all[rows, :], dkv_acc[rows, :].astype(BF16)], axis=1)
 
     def nothing(u):
@@ -294,19 +282,20 @@
     for acc in (dw1t_acc, dw2_acc):
         acc[...] = jnp.zeros_like(acc)
     ag_begin(N2)
+    wot_pad[:head, :] = jnp.zeros((head, width), BF16)
+    wot_pad[head:, :] = wo_ref[0]
+    wqkvt_pad[:head, :] = wqkvt_ref[:head, :]
+    wqkvt_pad[head:2 * head, :] = jnp.zeros((head, width), BF16)
+    wqkvt_pad[2 * head:, :] = wqkvt_ref[head:, :]
     for acc in (dwo_acc, dwqkvt_acc, dkv_acc):
         acc[...] = jnp.zeros_like(acc)
 
     def send_partner(u):
-        step = lax.div(u, 2)
-
-        @pl.when((lax.rem(u, 2) == 0) & (u > 0))
-        def _():
-            dx_copy(0, slot_of(step - 1, 0)).start()
-
-            @pl.when(step > 1)
-            def _():
-                dx_copy(0, slot_of(step - 1, 1)).start()
+        step, sub = lax.div(u - 1, 2), lax.rem(u - 1, 2)
+
+        @pl.when((u > 0) & ((sub == 0) | (step > 0)))
+        def _():
+            dx_copy(0, slot_of(step, sub)).start()
 
     def begin_n1(u):
         @pl.when(u == last_u - 3)
@@ -327,7 +316,7 @@
             join_partner(0, chips - u)
 
     def begin_rs(u):
-        @pl.when(u == last_u - 2)
+        @pl.when(u == last_u - 3)
         def _():
             ag_sent(N2)
             ag_sent(DY)
@@ -335,16 +324,14 @@
 
     ag_loop((N1,), join_first, qkv, begin_rs)
 
-    def forward_pair(u, carry):
+    def forward_chip(u, carry):
         @pl.when(u <= last_u - 3)
         def _():
             rs_tick(0, u)
 
-        def one(k, carry):
-            attend(jnp.where(k == 0, blocks - u, u - 1))
-            return carry
-        return lax.fori_loop(0, 2, one, carry)
-    lax.fori_loop(1, chips + 1, forward_pair, 0)
+        attend(chips - u)
+        return carry
+    lax.fori_loop(1, chips + 1, forward_chip, 0)
 
     for h in (0, 1):
         rows = pl.ds(h * H, H)
@@ -361,17 +348,19 @@
         j = chips - 1 - k
         chip = chip_of_slot(j)
         for core in (1 - c, c):
-            block = 2 * chip + core
-            part[block_rows(block), :] = dot_nt(grad_cols(block), wqkv_ref[...]).astype(BF16)
+            rows = block_rows(2 * chip + core)
+            part[rows, :] = dot_nn(grad_cols(rows), wqkvt_pad[...]).astype(BF16)
         dx_copy(1, j).start()
 
         @pl.when(k > 0)
         def _():
             join_partner(1, j + 1)
 
-        @pl.when(k == 3)
-        def _():
-            rs_begin(1)
+        for first in (1, 2):
+            @pl.when(k == 2 * first - 1)
+            def _():
+                for d in (0, 1):
+                    rs_copy(1, d, first, d if first == 1 else 1 - d).start()
         return carry
     lax.fori_loop(0, chips, share, 0)
     join_partner(1, 0)
@@ -380,17 +369,17 @@
         @pl.when(u <= last_u - 3)
         def _():
             rs_tick(1, u)
-        block = u - 1
-        cols_t = jnp.transpose(grad_cols(block).astype(F32)).astype(BF16)
-        dwqkvt_acc[...] += dot_nn(cols_t, n1_all[block_rows(block), :])
+        rows = ds_of(u - 1, pair)
+        cols_t = jnp.transpose(grad_cols(rows).astype(F32)).astype(BF16)
+        dwqkvt_acc[...] += dot_nn(cols_t, n1_all[rows, :])
         return carry
-    lax.fori_loop(1, blocks + 1, weight_block, 0)
+    lax.fori_loop(1, chips + 1, weight_block, 0)
 
     dw2_ref[...] = dw2_acc[...].astype(BF16)
     dw1_ref[...] = jnp.transpose(dw1t_acc[...]).astype(BF16)
     dwo_ref[0] = dwo_acc[...].astype(BF16)
-    dwqkv_t = jnp.concatenate([dwqkvt_acc[:head, :], dwqkvt_acc[2 * head:, :], jnp.zeros((head, width), F32)], axis=0)
-    dwqkv_ref[...] = jnp.transpose(dwqkv_t)[:, :3 * head].astype(BF16)
+    dwqkvt_ref[:head, :] = dwqkvt_acc[:head, :].astype(BF16)
+    dwqkvt_ref[head:, :] = dwqkvt_acc[2 * head:, :].astype(BF16)
 
     for h in (0, 1):
         rows = pl.ds(h * H, H)
@@ -401,6 +390,30 @@
     ag_sent(EG)
 
 
+def hand_over(arrays):
+    count = len(arrays)
+
+    def kernel(*refs):
+        ins, outs, held, sems = refs[:count], refs[count:2 * count], refs[2 * count:3 * count], refs[3 * count]
+        reads = [pltpu.make_async_copy(ins[k], held[k], sems.at[0, k]) for k in range(count)]
+        writes = [pltpu.make_async_copy(held[k], outs[k], sems.at[1, k]) for k in range(count)]
+        for read in reads:
+            read.start()
+        for read, write in zip(reads, writes):
+            read.wait()
+            write.start()
+        for write in writes:
+            write.wait()
+
+    return pl.pallas_call(
+        kernel,
+        out_shape=tuple(jax.ShapeDtypeStruct(a.shape, a.dtype) for a in arrays),
+        in_specs=[pl.BlockSpec(memory_space=pl.ANY)] * count,
+        out_specs=tuple([pl.BlockSpec(memory_space=pl.ANY)] * count),
+        scratch_shapes=[pltpu.VMEM(a.shape, a.dtype) for a in arrays] + [pltpu.SemaphoreType.DMA((2, count))],
+    )(*arrays)
+
+
 def solution(mesh):
     chips = mesh.shape['tp'] // 2
     row_spec = P(('dp', 'tp'), None)
@@ -413,30 +426,30 @@
         hidden = wfc1_loc.shape[1]
         tokens = 2 * chips * R
         half_ring = chips // 2
-        wqkv_pad = jnp.concatenate([wqkv_loc[:, :head], jnp.zeros_like(wqkv_loc[:, :head]), wqkv_loc[:, head:]], axis=1)
-        wout_pad = jnp.concatenate([jnp.zeros_like(wout_loc[0]), wout_loc[0]], axis=0)
         vm = pltpu.VMEM
         dma = pltpu.SemaphoreType.DMA
         scratch = [
             vm((tokens, width), BF16), vm((tokens, width), BF16), vm((tokens, width), BF16), vm((tokens, width), BF16),
             vm((chips, R, width), BF16), vm((2, half_ring, 2, R // 2, width), BF16),
-            vm((tokens, 2 * head), BF16), vm((8, 128), BF16), vm((tokens, 2 * head), BF16), vm((2 * head, tokens), BF16),
+            vm((tokens, 2 * head), BF16), vm((2 * head, width), BF16), vm((4 * head, width), BF16), vm((tokens, 2 * head), BF16), vm((2 * head, tokens), BF16),
             vm((head, tokens), F32), vm((1, tokens), F32),
             vm((tokens, 2 * head), BF16), vm((tokens, 2 * head), F32),
             vm((hidden, width), F32), vm((hidden, width), F32), vm((head, width), F32), vm((4 * head, width), F32), vm((R, width), F32),
             dma((4, 2, half_ring, 2)), dma((4, 2, half_ring, 2)), dma((4, chips, 2)), dma((4, chips, 2)),
             dma((2, 2, half_ring, 2)), dma((2, 2, half_ring, 2)), dma((2, chips)), dma((2, chips)),
         ]
-        return pl.pallas_call(
+        grads = pl.pallas_call(
             lambda *refs: layer_kernel(chips, *refs),
             out_shape=(
-                jax.ShapeDtypeStruct((R, width), BF16), jax.ShapeDtypeStruct((width, 3 * head), BF16),
+                jax.ShapeDtypeStruct((R, width), BF16), jax.ShapeDtypeStruct((3 * head, width), BF16),
                 jax.ShapeDtypeStruct((1, head, width), BF16), jax.ShapeDtypeStruct((width, hidden), BF16),
                 jax.ShapeDtypeStruct((hidden, width), BF16)),
             in_specs=[pl.BlockSpec(memory_space=pltpu.VMEM)] * 9,
             out_specs=tuple([pl.BlockSpec(memory_space=pltpu.VMEM)] * 5),
             scratch_shapes=scratch,
             compiler_params=pltpu.CompilerParams(collective_id=0, has_side_effects=True, vmem_limit_bytes=67043328),
-        )(in_rows, mid_rows, gout_rows, ln1_gain[None], ln2_gain[None], wqkv_pad, wout_pad, wfc1_loc, wfc2_loc)
+        )(in_rows, mid_rows, gout_rows, ln1_gain[None], ln2_gain[None], wqkv_loc.T, wout_loc, wfc1_loc, wfc2_loc)
+        grad_in, grad_wqkvt, grad_wout, grad_wfc1, grad_wfc2 = hand_over(grads)
+        return grad_in, grad_wqkvt.T, grad_wout, grad_wfc1, grad_wfc2
 
     return jax.shard_map(device_step, mesh=mesh, in_specs=in_specs, out_specs=out_specs, check_vma=False)

time: 306 us -> 278 us (0.908)
  Pallas kernels: 294 us -> 278 us
  local copies, waits for them, and re-layouts: 9.44 us -> 0 us
    pallas_call x1, Pallas kernels: 294 us -> 275 us  [device_step(): pl.pallas_call(lambda *refs: layer_kernel(chips, *refs), out_shape=(jax.S...]
    unnamed x16 -> x0, local copies, waits for them, and re-layouts: 4.75 us -> none
where the time goes in v3:
time: 278 us
  Pallas kernels  278 us (100%)
    pallas_call x1, Pallas kernels, device_step(): pl.pallas_call(lambda *refs: layer_kernel(chips, *refs), out_shape=(jax.S...  275 us

profile of v3, /device:TPU:21, one launch (start us, length us, event | category | flops | bytes accessed | tf_op | source)
XLA Modules:
  0.0 278.3 jit_solution(2418175851885465484)
XLA Ops:
  0.6 275.2 %shard_map.128 = (bf16[256,1024]{1,0:T(8,128)(2,1)}, bf16[192,1024]{1,0:T(8,128)(2,1)}, bf16[1,64,1024]{2,1,0:T(8,128)(2,1)}, bf16[1024,256]{1,0:T(8,128)(2,1)}, bf16[256,1024]{1,0:T(8,128)(2,1)}) custom-call(bf16[256,1024]{1,0:T(8,128)(2,1)} %refs_0_.1, bf16[256,1024]{1,0:T(8,128)(2,1)} %refs_1_.1, bf16[256,1024]{1,0:T(8,128)(2,1)} %refs_2_.1, ...), custom_call_target="tpu_custom_call" | custom-call | tf_op jit(solution)/shard_map/pallas_call | solution.py:441
  275.9 2.4 shard_map.129

commit v4 on v3

--- a/solution.py
+++ b/solution.py
@@ -64,6 +64,7 @@
     last_u = 2 * half_ring
     R, width = x_ref.shape
     H = R // 2
+    piece = R // 4
     head = dwo_ref.shape[1]
     pair = 2 * R
     full = (n2_all, dy_all, n1_all, dy_all)
@@ -76,6 +77,9 @@
 
     def half_rows(chip, core, h):
         return ds_of(2 * (2 * chip + core) + h, H)
+
+    def piece_rows(chip, core, q):
+        return ds_of(4 * (2 * chip + core) + q, piece)
 
     def block_rows(block):
         return ds_of(block, R)
@@ -108,12 +112,12 @@
                                             dx_recv.at[r, j], device_id={'tp': partner}, device_id_type=MESH)
 
     def rs_copy(r, d, s, h):
-        src = part.at[half_rows(chip_at(SIGN[d] * (half_ring - s + 1)), c, h)]
+        src = part.at[piece_rows(chip_at(SIGN[d] * (half_ring - s + 1)), c, h)]
         return pltpu.make_async_remote_copy(src, rbuf.at[d, s - 1, h], rs_send.at[r, d, s - 1, h],
                                             rs_recv.at[r, d, s - 1, h], device_id={'tp': nbr[d]}, device_id_type=MESH)
 
-    def ag_begin(a, src=None):
-        for h in (0, 1):
+    def ag_begin(a, src=None, halves=(0, 1)):
+        for h in halves:
             part_src = None if src is None else src.at[pl.ds(h * H, H)]
             for d in (0, 1):
                 ag_copy(a, d, 1, h, part_src).start()
@@ -158,34 +162,43 @@
             return carry
         lax.fori_loop(0, last_u + 1, body, 0)
 
-    def rs_begin(r):
+    def rs_first(r, s):
         for d in (0, 1):
-            rs_copy(r, d, 1, d).start()
-            rs_copy(r, d, 2, 1 - d).start()
-
-    def rs_tick(r, u):
-        s = 1 + lax.div(u, 2)
-        odd = lax.rem(u, 2)
+            for q in (0, 1):
+                rs_copy(r, d, s, (2 * d + q + 2 * (s - 1)) % 4).start()
+
+    def rs_tick(r, k):
+        s = 2 + lax.div(k + 2, 4)
+        place = lax.rem(k + 2, 4)
+        swapped = lax.rem(place + 2, 4)
+        rising = jnp.where(place == 3, 3, lax.rem(place + 2, 3))
+        order = (jnp.where(s == half_ring, place, jnp.where(s == half_ring - 1, rising, swapped)), place)
         for d in (0, 1):
-            h = jnp.where(odd == 1, d, 1 - d)
-            rs_copy(r, d, s, h).wait_recv()
-            rows = half_rows(chip_at(SIGN[d] * (half_ring - s)), c, h)
-            part[rows, :] = (part[rows, :].astype(F32) + rbuf[d, s - 1, h].astype(F32)).astype(BF16)
+            q = order[d]
+            rs_copy(r, d, s - 1, q).wait_recv()
+            rows = piece_rows(chip_at(SIGN[d] * (half_ring - s + 1)), c, q)
+            part[rows, :] = (part[rows, :].astype(F32) + rbuf[d, s - 2, q].astype(F32)).astype(BF16)
         for d in (0, 1):
-            rs_copy(r, d, s + 1, jnp.where(odd == 1, d, 1 - d)).start()
-
-    def rs_last(r, h):
+            rs_copy(r, d, s, order[d]).start()
+
+    def rs_ticks(r, u):
+        @pl.when(u <= last_u - 3)
+        def _():
+            rs_tick(r, 2 * u - 2)
+            rs_tick(r, 2 * u - 1)
+
+    def rs_last(r, q):
         for d in (0, 1):
-            rs_copy(r, d, half_ring, h).wait_recv()
-        own = part[half_rows(z, c, h), :].astype(F32)
-        return own + rbuf[0, half_ring - 1, h].astype(F32) + rbuf[1, half_ring - 1, h].astype(F32)
+            rs_copy(r, d, half_ring, q).wait_recv()
+        own = part[piece_rows(z, c, q), :].astype(F32)
+        return own + rbuf[0, half_ring - 1, q].astype(F32) + rbuf[1, half_ring - 1, q].astype(F32)
 
     def rs_sent(r):
         for d in (0, 1):
-            for h in (0, 1):
+            for q in range(4):
                 for s in range(1, half_ring + 1):
-                    if s > 1 or h == d:
-                        rs_copy(r, d, s, h).wait_send()
+                    if s > 1 or q // 2 == d:
+                        rs_copy(r, d, s, q).wait_send()
         for j in range(chips):
             dx_copy(r, j).wait_send()
 
@@ -233,36 +246,37 @@
         ot_all[:, rows] = acc / total
         lse_all[:, rows] = top + jnp.log(total)
 
-    def attend_grad(m):
-        rows = ds_of(m, pair)
-        e_rows = dy_all[rows, :]
+    def attend_grad(m, h):
+        rows = (half_rows(m, 0, h), half_rows(m, 1, h))
+        e_rows = jnp.concatenate([dy_all[k, :] for k in rows], axis=0)
         grads = dot_nt(e_rows, wot_pad[...]).astype(BF16)
         grads_t = jnp.transpose(grads.astype(F32))[head:]
-        out_t = ot_all[:, rows]
+        out_t = jnp.concatenate([ot_all[:, k] for k in rows], axis=1)
         dwo_acc[...] += dot_nn(out_t.astype(BF16), e_rows)
         row_dot = jnp.sum(grads_t * out_t, axis=0, keepdims=True)
-        both = jnp.concatenate([q_all[rows, :], grads], axis=0)
-        lse = lse_all[:, rows]
+        both = jnp.concatenate([q_all[k, :] for k in rows] + [grads], axis=0)
+        lse = jnp.concatenate([lse_all[:, k] for k in rows], axis=1)
 
         def tile(t, dqt, masked):
             keys = ds_of(t, pair)
             sr = dot_nt(kv_all[keys, :], both)
-            p = jnp.exp(sr[:, :pair] - lse)
+            p = jnp.exp(sr[:, :R] - lse)
             if masked:
-                p = jnp.where(keep_mask(p.shape), p, 0.0)
-            ds = (p * (sr[:, pair:] - row_dot)).astype(BF16)
+                query = lax.broadcasted_iota(jnp.int32, p.shape, 1)
+                query = jnp.where(query < H, query, query + H) + h * H
+                p = jnp.where(lax.broadcasted_iota(jnp.int32, p.shape, 0) <= query, p, 0.0)
+            ds = (p * (sr[:, R:] - row_dot)).astype(BF16)
             dkv_acc[keys, :] += dot_nn(jnp.concatenate([ds, p.astype(BF16)], axis=1), both)
             return dqt + dot_nn(kvt_all[:head, keys], ds)
 
-        dqt = lax.fori_loop(0, m, lambda t, k: tile(t, k, False), jnp.zeros((head, pair), F32))
+        dqt = lax.fori_loop(0, m, lambda t, k: tile(t, k, False), jnp.zeros((head, R), F32))
         dqt = tile(m, dqt, True) * (head ** -0.5)
-        dq_all[rows, :] = jnp.transpose(jnp.concatenate([dqt, jnp.zeros_like(dqt)], axis=0)).astype(BF16)
+        dq = jnp.transpose(jnp.concatenate([dqt, jnp.zeros_like(dqt)], axis=0)).astype(BF16)
+        dq_all[rows[0], :] = dq[:H]
+        dq_all[rows[1], :] = dq[H:]
 
     def grad_cols(rows):
         return jnp.concatenate([dq_all[rows, :], dkv_acc[rows, :].astype(BF16)], axis=1)
-
-    def nothing(u):
-        del u
 
     barrier = pltpu.get_barrier_semaphore()
     for peer in nbr + (partner,):
@@ -271,7 +285,6 @@
     ag_begin(DY, g_ref)
 
     def norm_rows(k, carry):
-        piece = H // 2
         src = ds_of(k, piece)
         dst = ds_of((2 * z + c) * 4 + k, piece)
         for raw, gain, out in ((h_ref, gain2_ref, n2_all), (x_ref, gain1_ref, n1_all)):
@@ -320,29 +333,56 @@
         def _():
             ag_sent(N2)
             ag_sent(DY)
-            rs_begin(0)
+            rs_first(0, 1)
+            rs_first(0, 2)
 
     ag_loop((N1,), join_first, qkv, begin_rs)
 
     def forward_chip(u, carry):
-        @pl.when(u <= last_u - 3)
-        def _():
-            rs_tick(0, u)
-
+        rs_ticks(0, u)
         attend(chips - u)
         return carry
     lax.fori_loop(1, chips + 1, forward_chip, 0)
 
-    for h in (0, 1):
-        rows = pl.ds(h * H, H)
+    def middle_piece(q, carry):
+        rows = ds_of(q, piece)
         mid_hat, mid_rstd = ln_forward(h_ref[rows, :].astype(F32))
-        grad = g_ref[rows, :].astype(F32) + ln_backward(mid_hat, mid_rstd, gain2_ref[...], rs_last(0, h))
+        grad = g_ref[rows, :].astype(F32) + ln_backward(mid_hat, mid_rstd, gain2_ref[...], rs_last(0, q))
         dh1[rows, :] = grad
-        dy_all[half_rows(z, c, h), :] = grad.astype(BF16)
+        dy_all[piece_rows(z, c, q), :] = grad.astype(BF16)
+        for h in (0, 1):
+            @pl.when(q == 2 * h + 1)
+            def _():
+                ag_begin(EG, halves=(h,))
+        return carry
+    lax.fori_loop(0, 4, middle_piece, 0)
     rs_sent(0)
-    ag_begin(EG)
-
-    ag_loop((EG,), nothing, attend_grad, nothing)
+
+    def backward_unit(v, carry):
+        s, h = 1 + lax.div(v, 2), lax.rem(v, 2)
+
+        @pl.when(v < last_u - 1)
+        def _():
+            for d in (0, 1):
+                g = jnp.where(s == half_ring, d, h)
+                ag_arrived(EG, d, s, g)
+
+                @pl.when((s < half_ring - 1) | ((s == half_ring - 1) & (h == d)))
+                def _():
+                    ag_copy(EG, d, s + 1, h).start()
+                dd_copy(EG, slot_of(s, d), chip_at(-SIGN[d] * s), c, g).start()
+
+        def one(sub, carry):
+            ends = (v == 0) | (v == last_u - 1)
+            step = jnp.where(v == 0, 0, jnp.where(v == last_u - 1, half_ring, 1 + lax.div(v - 1, 2)))
+            side = jnp.where(ends, 0, sub)
+            g = jnp.where(ends, sub, lax.rem(v + 1, 2))
+            chip = chip_at((2 * side - 1) * step)
+            dd_copy(EG, slot_of(step, side), chip, 1 - c, g).wait_recv()
+            attend_grad(chip, g)
+            return carry
+        return lax.fori_loop(0, 2, one, carry)
+    lax.fori_loop(0, last_u, backward_unit, 0)
 
     def share(k, carry):
         j = chips - 1 - k
@@ -359,16 +399,13 @@
         for first in (1, 2):
             @pl.when(k == 2 * first - 1)
             def _():
-                for d in (0, 1):
-                    rs_copy(1, d, first, d if first == 1 else 1 - d).start()
+                rs_first(1, first)
         return carry
     lax.fori_loop(0, chips, share, 0)
     join_partner(1, 0)
 
     def weight_block(u, carry):
-        @pl.when(u <= last_u - 3)
-        def _():
-            rs_tick(1, u)
+        rs_ticks(1, u)
         rows = ds_of(u - 1, pair)
         cols_t = jnp.transpose(grad_cols(rows).astype(F32)).astype(BF16)
         dwqkvt_acc[...] += dot_nn(cols_t, n1_all[rows, :])
@@ -381,10 +418,12 @@
     dwqkvt_ref[:head, :] = dwqkvt_acc[:head, :].astype(BF16)
     dwqkvt_ref[head:, :] = dwqkvt_acc[2 * head:, :].astype(BF16)
 
-    for h in (0, 1):
-        rows = pl.ds(h * H, H)
+    def final_piece(q, carry):
+        rows = ds_of(q, piece)
         in_hat, in_rstd = ln_forward(x_ref[rows, :].astype(F32))
-        dx_ref[rows, :] = (dh1[rows, :] + ln_backward(in_hat, in_rstd, gain1_ref[...], rs_last(1, h))).astype(BF16)
+        dx_ref[rows, :] = (dh1[rows, :] + ln_backward(in_hat, in_rstd, gain1_ref[...], rs_last(1, q))).astype(BF16)
+        return carry
+    lax.fori_loop(0, 4, final_piece, 0)
     rs_sent(1)
     ag_sent(N1)
     ag_sent(EG)
@@ -430,13 +469,13 @@
         dma = pltpu.SemaphoreType.DMA
         scratch = [
             vm((tokens, width), BF16), vm((tokens, width), BF16), vm((tokens, width), BF16), vm((tokens, width), BF16),
-            vm((chips, R, width), BF16), vm((2, half_ring, 2, R // 2, width), BF16),
+            vm((chips, R, width), BF16), vm((2, half_ring, 4, R // 4, width), BF16),
             vm((tokens, 2 * head), BF16), vm((2 * head, width), BF16), vm((4 * head, width), BF16), vm((tokens, 2 * head), BF16), vm((2 * head, tokens), BF16),
             vm((head, tokens), F32), vm((1, tokens), F32),
             vm((tokens, 2 * head), BF16), vm((tokens, 2 * head), F32),
             vm((hidden, width), F32), vm((hidden, width), F32), vm((head, width), F32), vm((4 * head, width), F32), vm((R, width), F32),
             dma((4, 2, half_ring, 2)), dma((4, 2, half_ring, 2)), dma((4, chips, 2)), dma((4, chips, 2)),
-            dma((2, 2, half_ring, 2)), dma((2, 2, half_ring, 2)), dma((2, chips)), dma((2, chips)),
+            dma((2, 2, half_ring, 4)), dma((2, 2, half_ring, 4)), dma((2, chips)), dma((2, chips)),
         ]
         grads = pl.pallas_call(
             lambda *refs: layer_kernel(chips, *refs),

time: 278 us -> 278 us (level)
  no operation moved by 1% of the time
where the time goes in v4:
time: 278 us
  Pallas kernels  277 us (100%)
    pallas_call x1, Pallas kernels, device_step(): pl.pallas_call(lambda *refs: layer_kernel(chips, *refs), out_shape=(jax.S...  275 us

profile of v4, /device:TPU:21, one launch (start us, length us, event | category | flops | bytes accessed | tf_op | source)
XLA Modules:
  0.0 278.0 jit_solution(6790320860016741966)
XLA Ops:
  0.6 274.9 %shard_map.128 = (bf16[256,1024]{1,0:T(8,128)(2,1)}, bf16[192,1024]{1,0:T(8,128)(2,1)}, bf16[1,64,1024]{2,1,0:T(8,128)(2,1)}, bf16[1024,256]{1,0:T(8,128)(2,1)}, bf16[256,1024]{1,0:T(8,128)(2,1)}) custom-call(bf16[256,1024]{1,0:T(8,128)(2,1)} %refs_0_.1, bf16[256,1024]{1,0:T(8,128)(2,1)} %refs_1_.1, bf16[256,1024]{1,0:T(8,128)(2,1)} %refs_2_.1, ...), custom_call_target="tpu_custom_call" | custom-call | tf_op jit(solution)/shard_map/pallas_call | solution.py:480
  275.5 2.4 shard_map.129

commit v5 on v4

--- a/solution.py
+++ b/solution.py
@@ -119,9 +119,9 @@
     def ag_begin(a, src=None, halves=(0, 1)):
         for h in halves:
             part_src = None if src is None else src.at[pl.ds(h * H, H)]
+            dd_copy(a, 0, z, c, h, part_src).start()
             for d in (0, 1):
                 ag_copy(a, d, 1, h, part_src).start()
-            dd_copy(a, 0, z, c, h, part_src).start()
 
     def ag_sent(a):
         for h in (0, 1):
@@ -144,11 +144,11 @@
                         @pl.when((s < half_ring) | (h == d))
                         def _():
                             ag_arrived(a, d, s, h)
+                            dd_copy(a, slot_of(s, d), chip_at(-SIGN[d] * s), c, h).start()
 
                             @pl.when((s < half_ring - 1) | ((s == half_ring - 1) & (h == d)))
                             def _():
                                 ag_copy(a, d, s + 1, h).start()
-                            dd_copy(a, slot_of(s, d), chip_at(-SIGN[d] * s), c, h).start()
             before(u)
 
             @pl.when((h == 0) | ((step > 0) & (step < half_ring)))
@@ -366,11 +366,11 @@
             for d in (0, 1):
                 g = jnp.where(s == half_ring, d, h)
                 ag_arrived(EG, d, s, g)
+                dd_copy(EG, slot_of(s, d), chip_at(-SIGN[d] * s), c, g).start()
 
                 @pl.when((s < half_ring - 1) | ((s == half_ring - 1) & (h == d)))
                 def _():
                     ag_copy(EG, d, s + 1, h).start()
-                dd_copy(EG, slot_of(s, d), chip_at(-SIGN[d] * s), c, g).start()
 
         def one(sub, carry):
             ends = (v == 0) | (v == last_u - 1)
@@ -412,6 +412,8 @@
         return carry
     lax.fori_loop(1, chips + 1, weight_block, 0)
 
+    ag_sent(N1)
+    ag_sent(EG)
     dw2_ref[...] = dw2_acc[...].astype(BF16)
     dw1_ref[...] = jnp.transpose(dw1t_acc[...]).astype(BF16)
     dwo_ref[0] = dwo_acc[...].astype(BF16)
@@ -425,8 +427,6 @@
         return carry
     lax.fori_loop(0, 4, final_piece, 0)
     rs_sent(1)
-    ag_sent(N1)
-    ag_sent(EG)
 
 
 def hand_over(arrays):

time: 278 us -> 278 us (level)
  no operation moved by 1% of the time
where the time goes in v5:
time: 278 us
  Pallas kernels  277 us (100%)
    pallas_call x1, Pallas kernels, device_step(): pl.pallas_call(lambda *refs: layer_kernel(chips, *refs), out_shape=(jax.S...  275 us

profile of v5, /device:TPU:21, one launch (start us, length us, event | category | flops | bytes accessed | tf_op | source)
XLA Modules:
  0.0 277.9 jit_solution(16374115031726950358)
XLA Ops:
  0.6 274.9 %shard_map.128 = (bf16[256,1024]{1,0:T(8,128)(2,1)}, bf16[192,1024]{1,0:T(8,128)(2,1)}, bf16[1,64,1024]{2,1,0:T(8,128)(2,1)}, bf16[1024,256]{1,0:T(8,128)(2,1)}, bf16[256,1024]{1,0:T(8,128)(2,1)}) custom-call(bf16[256,1024]{1,0:T(8,128)(2,1)} %refs_0_.1, bf16[256,1024]{1,0:T(8,128)(2,1)} %refs_1_.1, bf16[256,1024]{1,0:T(8,128)(2,1)} %refs_2_.1, ...), custom_call_target="tpu_custom_call" | custom-call | tf_op jit(solution)/shard_map/pallas_call | solution.py:480
  275.5 2.4 shard_map.129

commit v6 on v5

--- a/solution.py
+++ b/solution.py
@@ -53,8 +53,9 @@
     return lax.broadcasted_iota(jnp.int32, shape, 0) <= lax.broadcasted_iota(jnp.int32, shape, 1)
 
 
-def layer_kernel(chips, x_ref, h_ref, g_ref, gain1_ref, gain2_ref, wqkvt_ref, wo_ref, w1_ref, w2_ref,
-                 dx_ref, dwqkvt_ref, dwo_ref, dw1_ref, dw2_ref,
+def layer_kernel(chips, g_hbm, h_hbm, x_hbm, gain1_ref, gain2_ref, wqkvt_hbm, wo_hbm, w1_hbm, w2_hbm,
+                 dx_hbm, dwqkvt_hbm, dwo_hbm, dw1_hbm, dw2_hbm,
+                 g_ref, h_ref, x_ref, wqkvt_ref, wo_ref, w1_ref, w2_ref, dx_ref, dwqkvt_ref, dwo_ref, dw1_ref, dw2_ref, in_sem, out_sem,
                  n2_all, dy_all, n1_all, part, dbuf, rbuf, q_all, wot_pad, wqkvt_pad, kv_all, kvt_all, ot_all, lse_all,
                  dq_all, dkv_acc, dw1t_acc, dw2_acc, dwo_acc, dwqkvt_acc, dh1,
                  ag_send, ag_recv, dd_send, dd_recv, rs_send, rs_recv, dx_send, dx_recv):
@@ -62,10 +63,10 @@
     z, c = lax.div(me, 2), lax.rem(me, 2)
     half_ring = chips // 2
     last_u = 2 * half_ring
-    R, width = x_ref.shape
+    R, width = x_hbm.shape
     H = R // 2
     piece = R // 4
-    head = dwo_ref.shape[1]
+    head = dwo_hbm.shape[1]
     pair = 2 * R
     full = (n2_all, dy_all, n1_all, dy_all)
 
@@ -193,12 +194,14 @@
         own = part[piece_rows(z, c, q), :].astype(F32)
         return own + rbuf[0, half_ring - 1, q].astype(F32) + rbuf[1, half_ring - 1, q].astype(F32)
 
-    def rs_sent(r):
+    def rs_sent(r, steps):
         for d in (0, 1):
             for q in range(4):
-                for s in range(1, half_ring + 1):
+                for s in steps:
                     if s > 1 or q // 2 == d:
                         rs_copy(r, d, s, q).wait_send()
+
+    def dx_sent(r):
         for j in range(chips):
             dx_copy(r, j).wait_send()
 
@@ -278,11 +281,18 @@
     def grad_cols(rows):
         return jnp.concatenate([dq_all[rows, :], dkv_acc[rows, :].astype(BF16)], axis=1)
 
+    loads = [pltpu.make_async_copy(src, dst, in_sem.at[k]) for k, (src, dst) in enumerate((
+        (g_hbm, g_ref), (h_hbm, h_ref), (x_hbm, x_ref), (w1_hbm, w1_ref), (w2_hbm, w2_ref), (wqkvt_hbm, wqkvt_ref), (wo_hbm, wo_ref)))]
     barrier = pltpu.get_barrier_semaphore()
     for peer in nbr + (partner,):
         pl.semaphore_signal(barrier, inc=1, device_id={'tp': peer}, device_id_type=MESH)
+    for load in loads:
+        load.start()
     pl.semaphore_wait(barrier, 3)
+    loads[0].wait()
     ag_begin(DY, g_ref)
+    loads[1].wait()
+    loads[2].wait()
 
     def norm_rows(k, carry):
         src = ds_of(k, piece)
@@ -295,6 +305,8 @@
     for acc in (dw1t_acc, dw2_acc):
         acc[...] = jnp.zeros_like(acc)
     ag_begin(N2)
+    for load in loads[3:]:
+        load.wait()
     wot_pad[:head, :] = jnp.zeros((head, width), BF16)
     wot_pad[head:, :] = wo_ref[0]
     wqkvt_pad[:head, :] = wqkvt_ref[:head, :]
@@ -356,12 +368,14 @@
                 ag_begin(EG, halves=(h,))
         return carry
     lax.fori_loop(0, 4, middle_piece, 0)
-    rs_sent(0)
-
-    def backward_unit(v, carry):
+    rs_sent(0, range(1, half_ring + 1))
+    dx_sent(0)
+
+    def backward_call(x, carry):
+        v = lax.div(x - 1, 2)
         s, h = 1 + lax.div(v, 2), lax.rem(v, 2)
 
-        @pl.when(v < last_u - 1)
+        @pl.when((lax.rem(x, 2) == 1) & (v < last_u - 1))
         def _():
             for d in (0, 1):
                 g = jnp.where(s == half_ring, d, h)
@@ -372,17 +386,16 @@
                 def _():
                     ag_copy(EG, d, s + 1, h).start()
 
-        def one(sub, carry):
-            ends = (v == 0) | (v == last_u - 1)
-            step = jnp.where(v == 0, 0, jnp.where(v == last_u - 1, half_ring, 1 + lax.div(v - 1, 2)))
-            side = jnp.where(ends, 0, sub)
-            g = jnp.where(ends, sub, lax.rem(v + 1, 2))
-            chip = chip_at((2 * side - 1) * step)
-            dd_copy(EG, slot_of(step, side), chip, 1 - c, g).wait_recv()
-            attend_grad(chip, g)
-            return carry
-        return lax.fori_loop(0, 2, one, carry)
-    lax.fori_loop(0, last_u, backward_unit, 0)
+        first, final = x < 2, x >= 2 * last_u - 2
+        unit, side = lax.div(jnp.maximum(x - 2, 0), 2), lax.rem(x, 2)
+        step = jnp.where(first, 0, jnp.where(final, half_ring, 1 + lax.div(unit, 2)))
+        g = jnp.where(first | final, side, lax.rem(unit, 2))
+        side = jnp.where(first | final, 0, side)
+        chip = chip_at((2 * side - 1) * step)
+        dd_copy(EG, slot_of(step, side), chip, 1 - c, g).wait_recv()
+        attend_grad(chip, g)
+        return carry
+    lax.fori_loop(0, 2 * last_u, backward_call, 0)
 
     def share(k, carry):
         j = chips - 1 - k
@@ -412,21 +425,40 @@
         return carry
     lax.fori_loop(1, chips + 1, weight_block, 0)
 
-    ag_sent(N1)
-    ag_sent(EG)
     dw2_ref[...] = dw2_acc[...].astype(BF16)
     dw1_ref[...] = jnp.transpose(dw1t_acc[...]).astype(BF16)
     dwo_ref[0] = dwo_acc[...].astype(BF16)
     dwqkvt_ref[:head, :] = dwqkvt_acc[:head, :].astype(BF16)
     dwqkvt_ref[head:, :] = dwqkvt_acc[2 * head:, :].astype(BF16)
+    ag_sent(N1)
+    ag_sent(EG)
+    stores = [pltpu.make_async_copy(src, dst, out_sem.at[k]) for k, (src, dst) in enumerate((
+        (dw2_ref, dw2_hbm), (dw1_ref, dw1_hbm), (dwo_ref, dwo_hbm), (dwqkvt_ref, dwqkvt_hbm)))]
+    for store in stores:
+        store.start()
+    dx_sent(1)
+    rs_sent(1, range(1, half_ring))
+    for store in stores:
+        store.wait()
+
+    def dx_store(q):
+        rows = pl.ds(q * piece, piece)
+        return pltpu.make_async_copy(dx_ref.at[rows], dx_hbm.at[rows], out_sem.at[4 + q])
 
     def final_piece(q, carry):
         rows = ds_of(q, piece)
         in_hat, in_rstd = ln_forward(x_ref[rows, :].astype(F32))
         dx_ref[rows, :] = (dh1[rows, :] + ln_backward(in_hat, in_rstd, gain1_ref[...], rs_last(1, q))).astype(BF16)
+
+        @pl.when(q > 0)
+        def _():
+            dx_store(q - 1).start()
         return carry
     lax.fori_loop(0, 4, final_piece, 0)
-    rs_sent(1)
+    rs_sent(1, (half_ring,))
+    dx_store(3).start()
+    for q in range(4):
+        dx_store(q).wait()
 
 
 def hand_over(arrays):
@@ -434,14 +466,20 @@
 
     def kernel(*refs):
         ins, outs, held, sems = refs[:count], refs[count:2 * count], refs[2 * count:3 * count], refs[3 * count]
-        reads = [pltpu.make_async_copy(ins[k], held[k], sems.at[0, k]) for k in range(count)]
-        writes = [pltpu.make_async_copy(held[k], outs[k], sems.at[1, k]) for k in range(count)]
-        for read in reads:
+        moves = []
+        for k in range(count):
+            axis = len(arrays[k].shape) - 2
+            size = arrays[k].shape[axis] // 2
+            for h in (0, 1):
+                at = (slice(None),) * axis + (pl.ds(h * size, size),)
+                moves.append((pltpu.make_async_copy(ins[k].at[at], held[k].at[at], sems.at[0, k, h]),
+                              pltpu.make_async_copy(held[k].at[at], outs[k].at[at], sems.at[1, k, h])))
+        for read, _ in moves:
             read.start()
-        for read, write in zip(reads, writes):
+        for read, write in moves:
             read.wait()
             write.start()
-        for write in writes:
+        for _, write in moves:
             write.wait()
 
     return pl.pallas_call(
@@ -449,7 +487,7 @@
         out_shape=tuple(jax.ShapeDtypeStruct(a.shape, a.dtype) for a in arrays),
         in_specs=[pl.BlockSpec(memory_space=pl.ANY)] * count,
         out_specs=tuple([pl.BlockSpec(memory_space=pl.ANY)] * count),
-        scratch_shapes=[pltpu.VMEM(a.shape, a.dtype) for a in arrays] + [pltpu.SemaphoreType.DMA((2, count))],
+        scratch_shapes=[pltpu.VMEM(a.shape, a.dtype) for a in arrays] + [pltpu.SemaphoreType.DMA((2, count, 2))],
     )(*arrays)
 
 
@@ -466,8 +504,15 @@
         tokens = 2 * chips * R
         half_ring = chips // 2
         vm = pltpu.VMEM
+        hbm = pl.BlockSpec(memory_space=pl.ANY)
+        vmem = pl.BlockSpec(memory_space=pltpu.VMEM)
         dma = pltpu.SemaphoreType.DMA
-        scratch = [
+        outs = (
+            jax.ShapeDtypeStruct((R, width), BF16), jax.ShapeDtypeStruct((3 * head, width), BF16),
+            jax.ShapeDtypeStruct((1, head, width), BF16), jax.ShapeDtypeStruct((width, hidden), BF16),
+            jax.ShapeDtypeStruct((hidden, width), BF16))
+        wide = (in_rows, in_rows, in_rows, outs[1], wout_loc, wfc1_loc, wfc2_loc) + outs
+        scratch = [vm(a.shape, BF16) for a in wide] + [dma((7,)), dma((8,))] + [
             vm((tokens, width), BF16), vm((tokens, width), BF16), vm((tokens, width), BF16), vm((tokens, width), BF16),
             vm((chips, R, width), BF16), vm((2, half_ring, 4, R // 4, width), BF16),
             vm((tokens, 2 * head), BF16), vm((2 * head, width), BF16), vm((4 * head, width), BF16), vm((tokens, 2 * head), BF16), vm((2 * head, tokens), BF16),
@@ -479,15 +524,12 @@
         ]
         grads = pl.pallas_call(
             lambda *refs: layer_kernel(chips, *refs),
-            out_shape=(
-                jax.ShapeDtypeStruct((R, width), BF16), jax.ShapeDtypeStruct((3 * head, width), BF16),
-                jax.ShapeDtypeStruct((1, head, width), BF16), jax.ShapeDtypeStruct((width, hidden), BF16),
-                jax.ShapeDtypeStruct((hidden, width), BF16)),
-            in_specs=[pl.BlockSpec(memory_space=pltpu.VMEM)] * 9,
-            out_specs=tuple([pl.BlockSpec(memory_space=pltpu.VMEM)] * 5),
+            out_shape=outs,
+            in_specs=[hbm, hbm, hbm, vmem, vmem, hbm, hbm, hbm, hbm],
+            out_specs=(hbm,) * 5,
             scratch_shapes=scratch,
             compiler_params=pltpu.CompilerParams(collective_id=0, has_side_effects=True, vmem_limit_bytes=67043328),
-        )(in_rows, mid_rows, gout_rows, ln1_gain[None], ln2_gain[None], wqkv_loc.T, wout_loc, wfc1_loc, wfc2_loc)
+        )(gout_rows, mid_rows, in_rows, ln1_gain[None], ln2_gain[None], wqkv_loc.T, wout_loc, wfc1_loc, wfc2_loc)
         grad_in, grad_wqkvt, grad_wout, grad_wfc1, grad_wfc2 = hand_over(grads)
         return grad_in, grad_wqkvt.T, grad_wout, grad_wfc1, grad_wfc2
 

time: 278 us -> 273 us (0.982)
  Pallas kernels: 277 us -> 272 us
    pallas_call x1, Pallas kernels: 275 us -> 269 us  [device_step(): pl.pallas_call(lambda *refs: layer_kernel(chips, *refs), out_shape=outs,...]
where the time goes in v6:
time: 273 us; the launch traced here: 272 us
  Pallas kernels  272 us (100%)
    pallas_call x1, Pallas kernels, device_step(): pl.pallas_call(lambda *refs: layer_kernel(chips, *refs), out_shape=outs,...  269 us

profile of v6, /device:TPU:21, one launch (start us, length us, event | category | flops | bytes accessed | tf_op | source)
XLA Modules:
  0.0 272.5 jit_solution(9353968968296789653)
XLA Ops:
  0.6 269.4 %shard_map.128 = (bf16[256,1024]{1,0:T(8,128)(2,1)}, bf16[192,1024]{1,0:T(8,128)(2,1)}, bf16[1,64,1024]{2,1,0:T(8,128)(2,1)}, bf16[1024,256]{1,0:T(8,128)(2,1)}, bf16[256,1024]{1,0:T(8,128)(2,1)}) custom-call(bf16[256,1024]{1,0:T(8,128)(2,1)} %refs_0_.1, bf16[256,1024]{1,0:T(8,128)(2,1)} %refs_1_.1, bf16[256,1024]{1,0:T(8,128)(2,1)} %refs_2_.1, ...), custom_call_target="tpu_custom_call" | custom-call | tf_op jit(solution)/shard_map/pallas_call | solution.py:525
  270.1 2.4 shard_map.129

commit v7 on v6

--- a/solution.py
+++ b/solution.py
@@ -249,13 +249,13 @@
         ot_all[:, rows] = acc / total
         lse_all[:, rows] = top + jnp.log(total)
 
-    def attend_grad(m, h):
-        rows = (half_rows(m, 0, h), half_rows(m, 1, h))
+    def attend_grad(m, h=None):
+        rows = (ds_of(m, pair),) if h is None else (half_rows(m, 0, h), half_rows(m, 1, h))
+        count = pair if h is None else R
         e_rows = jnp.concatenate([dy_all[k, :] for k in rows], axis=0)
         grads = dot_nt(e_rows, wot_pad[...]).astype(BF16)
         grads_t = jnp.transpose(grads.astype(F32))[head:]
         out_t = jnp.concatenate([ot_all[:, k] for k in rows], axis=1)
-        dwo_acc[...] += dot_nn(out_t.astype(BF16), e_rows)
         row_dot = jnp.sum(grads_t * out_t, axis=0, keepdims=True)
         both = jnp.concatenate([q_all[k, :] for k in rows] + [grads], axis=0)
         lse = jnp.concatenate([lse_all[:, k] for k in rows], axis=1)
@@ -263,20 +263,21 @@
         def tile(t, dqt, masked):
             keys = ds_of(t, pair)
             sr = dot_nt(kv_all[keys, :], both)
-            p = jnp.exp(sr[:, :R] - lse)
+            p = jnp.exp(sr[:, :count] - lse)
             if masked:
                 query = lax.broadcasted_iota(jnp.int32, p.shape, 1)
-                query = jnp.where(query < H, query, query + H) + h * H
+                if h is not None:
+                    query = jnp.where(query < H, query, query + H) + h * H
                 p = jnp.where(lax.broadcasted_iota(jnp.int32, p.shape, 0) <= query, p, 0.0)
-            ds = (p * (sr[:, R:] - row_dot)).astype(BF16)
+            ds = (p * (sr[:, count:] - row_dot)).astype(BF16)
             dkv_acc[keys, :] += dot_nn(jnp.concatenate([ds, p.astype(BF16)], axis=1), both)
             return dqt + dot_nn(kvt_all[:head, keys], ds)
 
-        dqt = lax.fori_loop(0, m, lambda t, k: tile(t, k, False), jnp.zeros((head, R), F32))
+        dqt = lax.fori_loop(0, m, lambda t, k: tile(t, k, False), jnp.zeros((head, count), F32))
         dqt = tile(m, dqt, True) * (head ** -0.5)
         dq = jnp.transpose(jnp.concatenate([dqt, jnp.zeros_like(dqt)], axis=0)).astype(BF16)
-        dq_all[rows[0], :] = dq[:H]
-        dq_all[rows[1], :] = dq[H:]
+        for k, place in enumerate(rows):
+            dq_all[place, :] = dq[k * H:(k + 1) * H] if len(rows) > 1 else dq
 
     def grad_cols(rows):
         return jnp.concatenate([dq_all[rows, :], dkv_acc[rows, :].astype(BF16)], axis=1)
@@ -371,31 +372,36 @@
     rs_sent(0, range(1, half_ring + 1))
     dx_sent(0)
 
+    def e_tick(v):
+        s, h = 1 + lax.div(v, 2), lax.rem(v, 2)
+        for d in (0, 1):
+            g = jnp.where(s == half_ring, d, h)
+            ag_arrived(EG, d, s, g)
+            dd_copy(EG, slot_of(s, d), chip_at(-SIGN[d] * s), c, g).start()
+
+            @pl.when((s < half_ring - 1) | ((s == half_ring - 1) & (h == d)))
+            def _():
+                ag_copy(EG, d, s + 1, h).start()
+
     def backward_call(x, carry):
-        v = lax.div(x - 1, 2)
-        s, h = 1 + lax.div(v, 2), lax.rem(v, 2)
-
-        @pl.when((lax.rem(x, 2) == 1) & (v < last_u - 1))
-        def _():
-            for d in (0, 1):
-                g = jnp.where(s == half_ring, d, h)
-                ag_arrived(EG, d, s, g)
-                dd_copy(EG, slot_of(s, d), chip_at(-SIGN[d] * s), c, g).start()
-
-                @pl.when((s < half_ring - 1) | ((s == half_ring - 1) & (h == d)))
-                def _():
-                    ag_copy(EG, d, s + 1, h).start()
-
-        first, final = x < 2, x >= 2 * last_u - 2
+        @pl.when((lax.rem(x, 2) == 1) & (x < 2 * last_u - 3))
+        def _():
+            e_tick(lax.div(x - 1, 2))
+
         unit, side = lax.div(jnp.maximum(x - 2, 0), 2), lax.rem(x, 2)
-        step = jnp.where(first, 0, jnp.where(final, half_ring, 1 + lax.div(unit, 2)))
-        g = jnp.where(first | final, side, lax.rem(unit, 2))
-        side = jnp.where(first | final, 0, side)
+        step = jnp.where(x < 2, 0, 1 + lax.div(unit, 2))
+        g = jnp.where(x < 2, side, lax.rem(unit, 2))
+        side = jnp.where(x < 2, 0, side)
         chip = chip_at((2 * side - 1) * step)
         dd_copy(EG, slot_of(step, side), chip, 1 - c, g).wait_recv()
         attend_grad(chip, g)
         return carry
-    lax.fori_loop(0, 2 * last_u, backward_call, 0)
+    lax.fori_loop(0, 2 * last_u - 2, backward_call, 0)
+    e_tick(jnp.int32(last_u - 2))
+    last_chip = chip_at(half_ring)
+    for g in (0, 1):
+        dd_copy(EG, chips - 1, last_chip, 1 - c, g).wait_recv()
+    attend_grad(last_chip)
 
     def share(k, carry):
         j = chips - 1 - k
@@ -422,6 +428,7 @@
         rows = ds_of(u - 1, pair)
         cols_t = jnp.transpose(grad_cols(rows).astype(F32)).astype(BF16)
         dwqkvt_acc[...] += dot_nn(cols_t, n1_all[rows, :])
+        dwo_acc[...] += dot_nn(ot_all[:, rows].astype(BF16), dy_all[rows, :])
         return carry
     lax.fori_loop(1, chips + 1, weight_block, 0)
 

time: 273 us -> 272 us (level)
  no operation moved by 1% of the time
where the time goes in v7:
time: 272 us; the launch traced here: 271 us
  Pallas kernels  270 us (99%)
    pallas_call x1, Pallas kernels, device_step(): pl.pallas_call(lambda *refs: layer_kernel(chips, *refs), out_shape=outs,...  267 us

profile of v7, /device:TPU:21, one launch (start us, length us, event | category | flops | bytes accessed | tf_op | source)
XLA Modules:
  0.0 270.6 jit_solution(11077685360712759852)
XLA Ops:
  0.6 267.5 %shard_map.128 = (bf16[256,1024]{1,0:T(8,128)(2,1)}, bf16[192,1024]{1,0:T(8,128)(2,1)}, bf16[1,64,1024]{2,1,0:T(8,128)(2,1)}, bf16[1024,256]{1,0:T(8,128)(2,1)}, bf16[256,1024]{1,0:T(8,128)(2,1)}) custom-call(bf16[256,1024]{1,0:T(8,128)(2,1)} %refs_0_.1, bf16[256,1024]{1,0:T(8,128)(2,1)} %refs_1_.1, bf16[256,1024]{1,0:T(8,128)(2,1)} %refs_2_.1, ...), custom_call_target="tpu_custom_call" | custom-call | tf_op jit(solution)/shard_map/pallas_call | solution.py:532
  268.1 2.4 shard_map.129

commit v8 on v7

--- a/solution.py
+++ b/solution.py
@@ -260,8 +260,8 @@
         both = jnp.concatenate([q_all[k, :] for k in rows] + [grads], axis=0)
         lse = jnp.concatenate([lse_all[:, k] for k in rows], axis=1)
 
-        def tile(t, dqt, masked):
-            keys = ds_of(t, pair)
+        def tile(t, dqt, masked, size=pair):
+            keys = ds_of(t, size)
             sr = dot_nt(kv_all[keys, :], both)
             p = jnp.exp(sr[:, :count] - lse)
             if masked:
@@ -273,7 +273,13 @@
             dkv_acc[keys, :] += dot_nn(jnp.concatenate([ds, p.astype(BF16)], axis=1), both)
             return dqt + dot_nn(kvt_all[:head, keys], ds)
 
-        dqt = lax.fori_loop(0, m, lambda t, k: tile(t, k, False), jnp.zeros((head, count), F32))
+        dqt = jnp.zeros((head, count), F32)
+        done = 0
+        if h is not None:
+            twos = lax.div(m, 2)
+            dqt = lax.fori_loop(0, twos, lambda t, k: tile(t, k, False, 2 * pair), dqt)
+            done = 2 * twos
+        dqt = lax.fori_loop(done, m, lambda t, k: tile(t, k, False), dqt)
         dqt = tile(m, dqt, True) * (head ** -0.5)
         dq = jnp.transpose(jnp.concatenate([dqt, jnp.zeros_like(dqt)], axis=0)).astype(BF16)
         for k, place in enumerate(rows):

time: 272 us -> 271 us (level)
  no operation moved by 1% of the time
where the time goes in v8:
time: 271 us; the launch traced here: 269 us
  Pallas kernels  268 us (99%)
    pallas_call x1, Pallas kernels, device_step(): pl.pallas_call(lambda *refs: layer_kernel(chips, *refs), out_shape=outs,...  265 us

profile of v8, /device:TPU:21, one launch (start us, length us, event | category | flops | bytes accessed | tf_op | source)
XLA Modules:
  0.0 268.7 jit_solution(13775094796057651019)
XLA Ops:
  0.6 265.5 %shard_map.128 = (bf16[256,1024]{1,0:T(8,128)(2,1)}, bf16[192,1024]{1,0:T(8,128)(2,1)}, bf16[1,64,1024]{2,1,0:T(8,128)(2,1)}, bf16[1024,256]{1,0:T(8,128)(2,1)}, bf16[256,1024]{1,0:T(8,128)(2,1)}) custom-call(bf16[256,1024]{1,0:T(8,128)(2,1)} %refs_0_.1, bf16[256,1024]{1,0:T(8,128)(2,1)} %refs_1_.1, bf16[256,1024]{1,0:T(8,128)(2,1)} %refs_2_.1, ...), custom_call_target="tpu_custom_call" | custom-call | tf_op jit(solution)/shard_map/pallas_call | solution.py:538
  266.1 2.4 shard_map.129

commit v9 on v8

--- a/solution.py
+++ b/solution.py
@@ -390,7 +390,9 @@
                 ag_copy(EG, d, s + 1, h).start()
 
     def backward_call(x, carry):
-        @pl.when((lax.rem(x, 2) == 1) & (x < 2 * last_u - 3))
+        late = 2 * last_u - 6
+
+        @pl.when(((lax.rem(x, 2) == 1) & (x < 2 * last_u - 3) & (x != late - 1)) | (x == late))
         def _():
             e_tick(lax.div(x - 1, 2))
 

time: 271 us -> 272 us (level)
  Pallas kernels: 268 us -> 271 us
    pallas_call x1, Pallas kernels: 265 us -> 268 us  [device_step(): pl.pallas_call(lambda *refs: layer_kernel(chips, *refs), out_shape=outs,...]
where the time goes in v9:
time: 272 us
  Pallas kernels  271 us (100%)
    pallas_call x1, Pallas kernels, device_step(): pl.pallas_call(lambda *refs: layer_kernel(chips, *refs), out_shape=outs,...  268 us

profile of v9, /device:TPU:21, one launch (start us, length us, event | category | flops | bytes accessed | tf_op | source)
XLA Modules:
  0.0 271.5 jit_solution(7661160464402482761)
XLA Ops:
  0.6 268.3 %shard_map.128 = (bf16[256,1024]{1,0:T(8,128)(2,1)}, bf16[192,1024]{1,0:T(8,128)(2,1)}, bf16[1,64,1024]{2,1,0:T(8,128)(2,1)}, bf16[1024,256]{1,0:T(8,128)(2,1)}, bf16[256,1024]{1,0:T(8,128)(2,1)}) custom-call(bf16[256,1024]{1,0:T(8,128)(2,1)} %refs_0_.1, bf16[256,1024]{1,0:T(8,128)(2,1)} %refs_1_.1, bf16[256,1024]{1,0:T(8,128)(2,1)} %refs_2_.1, ...), custom_call_target="tpu_custom_call" | custom-call | tf_op jit(solution)/shard_map/pallas_call | solution.py:540
  268.9 2.4 shard_map.129
